TPU v7x, 64 devices: a 2x2x8 block of a 4x4x8 slice. The times are simulated.
64 devices in a mesh: prob: 4 (over x, y), feat: 16 (over z, core).
Axes of the slice: x: 2, y: 2, z: 8, core: 2. Of those that a mesh axis runs over, the one named last changes fastest.
The devices are a block of a 4x4x8 slice.
Arguments:
- x_data: bfloat16 [4096, 3072], P('prob'), parts along dimension 0
- targets: float32 [4096], P('prob'), parts along dimension 0
- w_in: float32 [8192, 3072], P(('prob', 'feat')), parts along dimension 0
- w_out: float32 [8192], P(('prob', 'feat')), parts along dimension 0
- reg_weight: float32 [4], P('prob'), parts along dimension 0
- step_size: float32 [4], P('prob'), parts along dimension 0
Outputs:
- output 1: float32 [8192, 3072], P(('prob', 'feat')), parts along dimension 0
- output 2: float32 [8192], P(('prob', 'feat')), parts along dimension 0
- output 3: float32 [24], P('prob'), parts along dimension 0
There are 4 independent parts. A program takes and returns all parts, laid end to end along the dimension named above; each array names one.
All inputs are finite; a program needn't handle non-finite values.
Results may differ from a plain program's by a relative error of at most 0.001.
Values are sent between devices in bfloat16 or wider.
A program may use at most 768 MiB of HBM per device.

v0:
```python
import math
import jax
import jax.numpy as jnp
from jax import lax
from jax.sharding import PartitionSpec as P

NUM_ITERS = 6
HIST_LEN = 3
FULL_PREC = lax.Precision.HIGHEST


def pair_dot_local(first, second):
    return jnp.sum(first[0] * second[0]) + jnp.sum(first[1] * second[1])


def pair_axpy(base, coef, other):
    return (base[0] + coef * other[0], base[1] + coef * other[1])


def two_loop(full_grad, hist_s, hist_y, rho_vals, gamma_scale, dot_fn):
    query_vec = full_grad
    a_coefs = {}
    for pos_idx in reversed(range(len(hist_s))):
        a_coefs[pos_idx] = rho_vals[pos_idx] * dot_fn(hist_s[pos_idx], query_vec)
        query_vec = pair_axpy(query_vec, -a_coefs[pos_idx], hist_y[pos_idx])
    result = (gamma_scale * query_vec[0], gamma_scale * query_vec[1])
    for pos_idx in range(len(hist_s)):
        b_coef = rho_vals[pos_idx] * dot_fn(hist_y[pos_idx], result)
        result = pair_axpy(result, a_coefs[pos_idx] - b_coef, hist_s[pos_idx])
    return result


def global_dot(first, second):
    return lax.psum(pair_dot_local(first, second), "feat")


def solution(mesh):
    feat_size = mesh.shape["feat"]

    def local_solve(x_loc, t_loc, win_loc, wout_loc, reg_loc, step_loc):
        num_rows = x_loc.shape[0]
        in_scale = 1.0 / math.sqrt(x_loc.shape[1])
        out_scale = 1.0 / math.sqrt(win_loc.shape[0] * feat_size)
        reg_coef = reg_loc[0]
        step_coef = step_loc[0]
        x_f32 = x_loc.astype(jnp.float32)
        params = (win_loc, wout_loc)
        prev_params = params
        prev_grad = params
        hist_s = []
        hist_y = []
        rho_vals = []
        losses = []
        for iter_idx in range(NUM_ITERS):
            pre_act = lax.dot_general(x_f32, params[0], (((1,), (1,)), ((), ())), precision=FULL_PREC) * in_scale
            hid_act = jnp.tanh(pre_act)
            part_logits = jnp.dot(hid_act, params[1], precision=FULL_PREC) * out_scale
            logits = lax.psum(part_logits, "feat")
            losses.append(jnp.mean(jax.nn.softplus(logits) - t_loc * logits))
            resid_vec = (jax.nn.sigmoid(logits) - t_loc) / num_rows
            grad_out = jnp.dot(resid_vec, hid_act, precision=FULL_PREC) * out_scale
            d_pre = resid_vec[:, None] * (params[1] * (out_scale * in_scale))[None, :] * (1.0 - hid_act * hid_act)
            grad_in = lax.dot_general(d_pre, x_f32, (((0,), (0,)), ((), ())), precision=FULL_PREC)
            full_grad = (grad_in + reg_coef * params[0], grad_out + reg_coef * params[1])
            if iter_idx == 0:
                direction = full_grad
            else:
                s_vec = pair_axpy(params, -1.0, prev_params)
                y_vec = pair_axpy(full_grad, -1.0, prev_grad)
                curv_pair = lax.psum(jnp.stack([pair_dot_local(y_vec, s_vec), pair_dot_local(y_vec, y_vec)]), "feat")
                hist_s = (hist_s + [s_vec])[-HIST_LEN:]
                hist_y = (hist_y + [y_vec])[-HIST_LEN:]
                rho_vals = (rho_vals + [1.0 / curv_pair[0]])[-HIST_LEN:]
                gamma_scale = curv_pair[0] / curv_pair[1]
                direction = two_loop(full_grad, hist_s, hist_y, rho_vals, gamma_scale, global_dot)
            prev_params = params
            prev_grad = full_grad
            params = pair_axpy(params, -step_coef, direction)
        return params[0], params[1], jnp.stack(losses)

    specs_in = (P("prob", None), P("prob"), P(("prob", "feat"), None), P(("prob", "feat")), P("prob"), P("prob"))
    specs_out = (P(("prob", "feat"), None), P(("prob", "feat")), P("prob"))
    return jax.shard_map(local_solve, mesh=mesh, in_specs=specs_in, out_specs=specs_out, check_vma=False)
```

profile of v0, /device:TPU:21, one launch (start us, length us, event | category | flops | bytes accessed | tf_op | source)
XLA Modules:
  0.0 1008.3 jit_solution(13963738360160483793)
XLA Ops:
  2.0 8.4 fusion
  10.9 28.8 %psum.245 = f32[1024]{0:T(1024)S(1)} all-reduce(f32[1024]{0:T(1024)S(1)} %broadcast_multiply_fusion.5), channel_id=1, replica_groups=mesh['prob'=4,'feat'=16] {'feat'}, use_global_device_ids=true, to_apply=%region_0.0 | all-reduce | flops 1024 | bytes 8192 | tf_op jit(solution)/shard_map/psum | solution.py:58
  40.2 7.2 multiply_add_fusion.29
  47.3 5.1 fusion.2
  53.0 26.1 %psum.246 = f32[1024]{0:T(1024)S(1)} all-reduce(f32[1024]{0:T(1024)S(1)} %broadcast_multiply_fusion.4), channel_id=1, replica_groups=mesh['prob'=4,'feat'=16] {'feat'}, use_global_device_ids=true, to_apply=%region_1.2 | all-reduce | flops 1024 | bytes 8192 | tf_op jit(solution)/shard_map/psum | solution.py:58
  80.1 9.4 multiply_reduce_fusion.31
  93.3 24.1 %all-reduce.4 = (f32[2]{0:T(128)S(1)}, f32[]{:T(128)}) all-reduce(f32[2]{0:T(128)S(1)} %pad_maximum_fusion, f32[]{:T(128)S(6)} %add.499), channel_id=1, replica_groups=mesh['prob'=4,'feat'=16] {'feat'}, use_global_device_ids=true, to_apply=%region_6.7 | all-reduce | flops 3 | bytes 24 | tf_op jit(solution)/shard_map/psum | solution.py:70
  121.1 2.5 multiply_reduce_fusion.30
  124.7 24.2 %psum.249 = f32[]{:T(128)} all-reduce(f32[]{:T(128)S(6)} %add.502), channel_id=1, replica_groups=mesh['prob'=4,'feat'=16] {'feat'}, use_global_device_ids=true, to_apply=%region_12.13 | all-reduce | flops 1 | bytes 8 | tf_op jit(solution)/shard_map/psum | solution.py:34
  152.0 7.8 fusion.4
  160.4 23.6 %psum.250 = f32[1024]{0:T(1024)S(1)} all-reduce(f32[1024]{0:T(1024)S(1)} %broadcast_multiply_fusion.3), channel_id=1, replica_groups=mesh['prob'=4,'feat'=16] {'feat'}, use_global_device_ids=true, to_apply=%region_13.14 | all-reduce | flops 1024 | bytes 8192 | tf_op jit(solution)/shard_map/psum | solution.py:58
  185.0 10.0 multiply_reduce_fusion.27
  198.7 24.5 %all-reduce.3 = (f32[2]{0:T(128)S(1)}, f32[]{:T(128)}) all-reduce(f32[2]{0:T(128)S(1)} %pad_maximum_fusion.1, f32[]{:T(128)S(6)} %add.516), channel_id=1, replica_groups=mesh['prob'=4,'feat'=16] {'feat'}, use_global_device_ids=true, to_apply=%region_18.19 | all-reduce | flops 3 | bytes 24 | tf_op jit(solution)/shard_map/psum | solution.py:70
  227.0 4.0 multiply_reduce_fusion.26
  232.3 24.1 %psum.253 = f32[]{:T(128)} all-reduce(f32[]{:T(128)S(6)} %add.519), channel_id=1, replica_groups=mesh['prob'=4,'feat'=16] {'feat'}, use_global_device_ids=true, to_apply=%region_24.25 | all-reduce | flops 1 | bytes 8 | tf_op jit(solution)/shard_map/psum | solution.py:34
  257.1 2.4 multiply_reduce_fusion.25
  261.4 24.1 %psum.254 = f32[]{:T(128)} all-reduce(f32[]{:T(128)S(6)} %add.522), channel_id=1, replica_groups=mesh['prob'=4,'feat'=16] {'feat'}, use_global_device_ids=true, to_apply=%region_27.28 | all-reduce | flops 1 | bytes 8 | tf_op jit(solution)/shard_map/psum | solution.py:34
  286.2 4.1 multiply_reduce_fusion.24
  292.3 24.1 %psum.255 = f32[]{:T(128)} all-reduce(f32[]{:T(128)S(6)} %add.525), channel_id=1, replica_groups=mesh['prob'=4,'feat'=16] {'feat'}, use_global_device_ids=true, to_apply=%region_30.31 | all-reduce | flops 1 | bytes 8 | tf_op jit(solution)/shard_map/psum | solution.py:34
  317.1 4.2 multiply_add_fusion.21
  321.6 5.1 fusion.6
  327.2 23.6 %psum.256 = f32[1024]{0:T(1024)S(1)} all-reduce(f32[1024]{0:T(1024)S(1)} %broadcast_multiply_fusion.2), channel_id=1, replica_groups=mesh['prob'=4,'feat'=16] {'feat'}, use_global_device_ids=true, to_apply=%region_31.32 | all-reduce | flops 1024 | bytes 8192 | tf_op jit(solution)/shard_map/psum | solution.py:58
  351.9 10.1 %multiply_reduce_fusion.21 = (f32[]{:T(128)}, f32[]{:T(128)}, f32[]{:T(128)}, f32[128,3072]{1,0:T(8,128)S(1)}, f32[128,3072]{1,0:T(8,128)}, /*index=5*/f32[128,3072]{1,0:T(8,128)}) fusion(f32[128,3072]{1,0:T(8,128)} %get-tuple-element.126, f32[128,3072]{1,0:T(8,128)} %copy-done.16, f32[128,3072]{1,0:T(8,128)} %copy-done.17, f32[]{:T(128)} %bitcast.144, ...), kind=kOutput, calls=%fused_computation.49 | convolution fusion | flops 4837081088 | bytes 16257552 | tf_op jit(solution)/shard_map/dot_general | solution.py:63
  365.9 24.1 %all-reduce.2 = (f32[2]{0:T(128)S(1)}, f32[]{:T(128)}) all-reduce(f32[2]{0:T(128)S(1)} %pad_maximum_fusion.2, f32[]{:T(128)S(6)} %add.539), channel_id=1, replica_groups=mesh['prob'=4,'feat'=16] {'feat'}, use_global_device_ids=true, to_apply=%region_36.37 | all-reduce | flops 3 | bytes 24 | tf_op jit(solution)/shard_map/psum | solution.py:70
  396.2 24.3 %psum.259 = f32[]{:T(128)} all-reduce(f32[]{:T(128)S(6)} %add.542), channel_id=1, replica_groups=mesh['prob'=4,'feat'=16] {'feat'}, use_global_device_ids=true, to_apply=%region_42.43 | all-reduce | flops 1 | bytes 8 | tf_op jit(solution)/shard_map/psum | solution.py:34
  423.0 4.8 multiply_reduce_fusion.19
  429.0 24.1 %psum.260 = f32[]{:T(128)} all-reduce(f32[]{:T(128)S(6)} %add.545), channel_id=1, replica_groups=mesh['prob'=4,'feat'=16] {'feat'}, use_global_device_ids=true, to_apply=%region_45.46 | all-reduce | flops 1 | bytes 8 | tf_op jit(solution)/shard_map/psum | solution.py:34
  453.8 2.5 multiply_reduce_fusion.18
  458.1 24.1 %psum.261 = f32[]{:T(128)} all-reduce(f32[]{:T(128)S(6)} %add.548), channel_id=1, replica_groups=mesh['prob'=4,'feat'=16] {'feat'}, use_global_device_ids=true, to_apply=%region_48.49 | all-reduce | flops 1 | bytes 8 | tf_op jit(solution)/shard_map/psum | solution.py:34
  482.9 4.0 multiply_reduce_fusion.17
  488.9 24.1 %psum.262 = f32[]{:T(128)} all-reduce(f32[]{:T(128)S(6)} %add.551), channel_id=1, replica_groups=mesh['prob'=4,'feat'=16] {'feat'}, use_global_device_ids=true, to_apply=%region_51.52 | all-reduce | flops 1 | bytes 8 | tf_op jit(solution)/shard_map/psum | solution.py:34
  513.7 3.5 multiply_reduce_fusion.16
  519.1 24.1 %psum.263 = f32[]{:T(128)} all-reduce(f32[]{:T(128)S(6)} %add.554), channel_id=1, replica_groups=mesh['prob'=4,'feat'=16] {'feat'}, use_global_device_ids=true, to_apply=%region_54.55 | all-reduce | flops 1 | bytes 8 | tf_op jit(solution)/shard_map/psum | solution.py:34
  543.9 3.5 multiply_add_fusion.14
  548.0 5.1 fusion.8
  553.6 23.6 %psum.264 = f32[1024]{0:T(1024)S(1)} all-reduce(f32[1024]{0:T(1024)S(1)} %broadcast_multiply_fusion.1), channel_id=1, replica_groups=mesh['prob'=4,'feat'=16] {'feat'}, use_global_device_ids=true, to_apply=%region_55.56 | all-reduce | flops 1024 | bytes 8192 | tf_op jit(solution)/shard_map/psum | solution.py:58
  578.4 10.5 %multiply_reduce_fusion.13 = (f32[]{:T(128)}, f32[]{:T(128)}, f32[]{:T(128)}, f32[128,3072]{1,0:T(8,128)}, f32[128,3072]{1,0:T(8,128)}, /*index=5*/f32[128,3072]{1,0:T(8,128)}) fusion(f32[128,3072]{1,0:T(8,128)} %get-tuple-element.128, f32[128,3072]{1,0:T(8,128)} %copy-done.13, f32[128,3072]{1,0:T(8,128)} %copy-done.16, f32[]{:T(128)} %bitcast.143, ...), kind=kOutput, calls=%fused_computation.33 | convolution fusion | flops 4837081088 | bytes 16257552 | tf_op jit(solution)/shard_map/dot_general | solution.py:63
  592.9 24.3 %all-reduce.1 = (f32[2]{0:T(128)S(1)}, f32[]{:T(128)}) all-reduce(f32[2]{0:T(128)S(1)} %pad_maximum_fusion.3, f32[]{:T(128)S(6)} %add.568), channel_id=1, replica_groups=mesh['prob'=4,'feat'=16] {'feat'}, use_global_device_ids=true, to_apply=%region_60.61 | all-reduce | flops 3 | bytes 24 | tf_op jit(solution)/shard_map/psum | solution.py:70
  619.7 3.0 multiply_reduce_fusion.12
  624.1 24.1 %psum.267 = f32[]{:T(128)} all-reduce(f32[]{:T(128)S(6)} %add.571), channel_id=1, replica_groups=mesh['prob'=4,'feat'=16] {'feat'}, use_global_device_ids=true, to_apply=%region_66.67 | all-reduce | flops 1 | bytes 8 | tf_op jit(solution)/shard_map/psum | solution.py:34
  650.7 4.5 multiply_reduce_fusion.11
  656.5 24.1 %psum.268 = f32[]{:T(128)} all-reduce(f32[]{:T(128)S(6)} %add.574), channel_id=1, replica_groups=mesh['prob'=4,'feat'=16] {'feat'}, use_global_device_ids=true, to_apply=%region_69.70 | all-reduce | flops 1 | bytes 8 | tf_op jit(solution)/shard_map/psum | solution.py:34
  681.3 3.0 multiply_reduce_fusion.10
  686.3 24.1 %psum.269 = f32[]{:T(128)} all-reduce(f32[]{:T(128)S(6)} %add.577), channel_id=1, replica_groups=mesh['prob'=4,'feat'=16] {'feat'}, use_global_device_ids=true, to_apply=%region_72.73 | all-reduce | flops 1 | bytes 8 | tf_op jit(solution)/shard_map/psum | solution.py:34
  711.1 4.0 multiply_reduce_fusion.9
  716.9 24.1 %psum.270 = f32[]{:T(128)} all-reduce(f32[]{:T(128)S(6)} %add.580), channel_id=1, replica_groups=mesh['prob'=4,'feat'=16] {'feat'}, use_global_device_ids=true, to_apply=%region_75.76 | all-reduce | flops 1 | bytes 8 | tf_op jit(solution)/shard_map/psum | solution.py:34
  741.7 3.5 multiply_reduce_fusion.8
  747.0 24.1 %psum.271 = f32[]{:T(128)} all-reduce(f32[]{:T(128)S(6)} %add.583), channel_id=1, replica_groups=mesh['prob'=4,'feat'=16] {'feat'}, use_global_device_ids=true, to_apply=%region_78.79 | all-reduce | flops 1 | bytes 8 | tf_op jit(solution)/shard_map/psum | solution.py:34
  771.8 3.5 multiply_add_fusion.7
  775.8 5.1 fusion.10
  781.5 23.9 %psum.272 = f32[1024]{0:T(1024)S(1)} all-reduce(f32[1024]{0:T(1024)S(1)} %broadcast_multiply_fusion), channel_id=1, replica_groups=mesh['prob'=4,'feat'=16] {'feat'}, use_global_device_ids=true, to_apply=%region_79.80 | all-reduce | flops 1024 | bytes 8192 | tf_op jit(solution)/shard_map/psum | solution.py:58
  811.4 9.4 multiply_reduce_fusion.5
  824.6 24.1 %all-reduce = (f32[2]{0:T(128)S(1)}, f32[]{:T(128)}) all-reduce(f32[2]{0:T(128)S(1)} %pad_maximum_fusion.4, f32[]{:T(128)S(6)} %add.597), channel_id=1, replica_groups=mesh['prob'=4,'feat'=16] {'feat'}, use_global_device_ids=true, to_apply=%region_84.85 | all-reduce | flops 3 | bytes 24 | tf_op jit(solution)/shard_map/psum | solution.py:70
  851.2 3.0 multiply_reduce_fusion.4
  855.6 24.1 %psum.275 = f32[]{:T(128)} all-reduce(f32[]{:T(128)S(6)} %add.600), channel_id=1, replica_groups=mesh['prob'=4,'feat'=16] {'feat'}, use_global_device_ids=true, to_apply=%region_90.91 | all-reduce | flops 1 | bytes 8 | tf_op jit(solution)/shard_map/psum | solution.py:34
  882.2 4.7 multiply_reduce_fusion.3
  888.3 24.1 %psum.276 = f32[]{:T(128)} all-reduce(f32[]{:T(128)S(6)} %add.603), channel_id=1, replica_groups=mesh['prob'=4,'feat'=16] {'feat'}, use_global_device_ids=true, to_apply=%region_93.94 | all-reduce | flops 1 | bytes 8 | tf_op jit(solution)/shard_map/psum | solution.py:34
  913.1 2.4 multiply_reduce_fusion.2
  917.5 24.1 %psum.277 = f32[]{:T(128)} all-reduce(f32[]{:T(128)S(6)} %add.606), channel_id=1, replica_groups=mesh['prob'=4,'feat'=16] {'feat'}, use_global_device_ids=true, to_apply=%region_96.97 | all-reduce | flops 1 | bytes 8 | tf_op jit(solution)/shard_map/psum | solution.py:34
  942.3 4.0 multiply_reduce_fusion.1
  948.2 24.1 %psum.278 = f32[]{:T(128)} all-reduce(f32[]{:T(128)S(6)} %add.609), channel_id=1, replica_groups=mesh['prob'=4,'feat'=16] {'feat'}, use_global_device_ids=true, to_apply=%region_99.100 | all-reduce | flops 1 | bytes 8 | tf_op jit(solution)/shard_map/psum | solution.py:34
  973.0 4.1 multiply_reduce_fusion
  979.0 24.1 %psum.279 = f32[]{:T(128)} all-reduce(f32[]{:T(128)S(6)} %add.612), channel_id=1, replica_groups=mesh['prob'=4,'feat'=16] {'feat'}, use_global_device_ids=true, to_apply=%region_102.103 | all-reduce | flops 1 | bytes 8 | tf_op jit(solution)/shard_map/psum | solution.py:34
  1003.8 3.6 multiply_add_fusion
  (135 shorter events, 32.4 us)
Async XLA Ops:
  1.9 8.5 copy-start.26
  1.9 37.8 %copy-start.25 = (f32[1024]{0:T(1024)S(1)}, f32[1024]{0:T(1024)}, u32[]{:S(2)}) copy-start(f32[1024]{0:T(1024)} %param.7) | copy-start | bytes 12292
  1.9 38.2 %copy-start.20 = (f32[128,3072]{1,0:T(8,128)S(1)}, f32[128,3072]{1,0:T(8,128)}, u32[]{:S(2)}) copy-start(f32[128,3072]{1,0:T(8,128)} %param.8) | copy-start | bytes 4718596
  39.8 7.6 slice-start
  40.2 7.2 slice-start.1
  47.3 5.1 copy-start.15
  52.4 27.7 %copy-start.24 = (f32[1024,128]{1,0:T(8,128)}, f32[1024,128]{1,0:T(8,128)S(1)}, u32[]{:S(2)}) copy-start(f32[1024,128]{1,0:T(8,128)S(1)} %fusion.2) | copy-start | bytes 1572868
  89.5 60.1 %copy-start.12 = (f32[128,3072]{1,0:T(8,128)}, f32[128,3072]{1,0:T(8,128)S(1)}, u32[]{:S(2)}) copy-start(f32[128,3072]{1,0:T(8,128)S(1)} %get-tuple-element.106) | copy-start | bytes 4718596
  89.5 167.5 %copy-start.3 = (f32[128,3072]{1,0:T(8,128)}, f32[128,3072]{1,0:T(8,128)S(1)}, u32[]{:S(2)}) copy-start(f32[128,3072]{1,0:T(8,128)S(1)} %get-tuple-element.105) | copy-start | bytes 4718596
  152.0 7.8 copy-start.17
  159.8 25.2 %copy-start.21 = (f32[1024,128]{1,0:T(8,128)}, f32[1024,128]{1,0:T(8,128)S(1)}, u32[]{:S(2)}) copy-start(f32[1024,128]{1,0:T(8,128)S(1)} %fusion.4) | copy-start | bytes 1572868
  195.0 36.0 %copy-start.9 = (f32[128,3072]{1,0:T(8,128)}, f32[128,3072]{1,0:T(8,128)S(1)}, u32[]{:S(2)}) copy-start(f32[128,3072]{1,0:T(8,128)S(1)} %get-tuple-element.99) | copy-start | bytes 4718596
  286.2 35.0 %slice-start.2 = ((s8[6291456]{0:T(1024)(128)(4,1)}), s8[2097152]{0:T(1024)(128)(4,1)S(1)}, s32[]{:S(2)}) async-start(s8[6291456]{0:T(1024)(128)(4,1)} %bitcast.154), calls=%async_computation.2 | async-start | bytes 4194304
  317.1 4.5 slice-start.3
  321.2 5.4 copy-start.16
  326.6 25.3 %copy-start.22 = (f32[1024,128]{1,0:T(8,128)}, f32[1024,128]{1,0:T(8,128)S(1)}, u32[]{:S(2)}) copy-start(f32[1024,128]{1,0:T(8,128)S(1)} %fusion.6) | copy-start | bytes 1572868
  351.9 40.6 %copy-start.7 = (f32[128,3072]{1,0:T(8,128)S(1)}, f32[128,3072]{1,0:T(8,128)}, u32[]{:S(2)}) copy-start(f32[128,3072]{1,0:T(8,128)} %get-tuple-element.100) | copy-start | bytes 4718596
  362.0 61.0 %copy-start = (f32[128,3072]{1,0:T(8,128)}, f32[128,3072]{1,0:T(8,128)S(1)}, u32[]{:S(2)}) copy-start(f32[128,3072]{1,0:T(8,128)S(1)} %get-tuple-element.89) | copy-start | bytes 4718596
  423.0 30.8 %copy-start.4 = (f32[128,3072]{1,0:T(8,128)S(1)}, f32[128,3072]{1,0:T(8,128)}, u32[]{:S(2)}) copy-start(f32[128,3072]{1,0:T(8,128)} %copy-done.3) | copy-start | bytes 4718596
  453.8 29.1 %copy-start.10 = (f32[128,3072]{1,0:T(8,128)S(1)}, f32[128,3072]{1,0:T(8,128)}, u32[]{:S(2)}) copy-start(f32[128,3072]{1,0:T(8,128)} %copy-done.9) | copy-start | bytes 4718596
  513.7 33.8 %slice-start.4 = ((s8[6291456]{0:T(1024)(128)(4,1)}), s8[2097152]{0:T(1024)(128)(4,1)S(1)}, s32[]{:S(2)}) async-start(s8[6291456]{0:T(1024)(128)(4,1)} %bitcast.156), calls=%async_computation.4 | async-start | bytes 4194304
  543.9 4.1 slice-start.5
  547.4 5.6 copy-start.13
  553.1 25.3 %copy-start.23 = (f32[1024,128]{1,0:T(8,128)}, f32[1024,128]{1,0:T(8,128)S(1)}, u32[]{:S(2)}) copy-start(f32[1024,128]{1,0:T(8,128)S(1)} %fusion.8) | copy-start | bytes 1572868
  578.4 41.4 %copy-start.5 = (f32[128,3072]{1,0:T(8,128)S(1)}, f32[128,3072]{1,0:T(8,128)}, u32[]{:S(2)}) copy-start(f32[128,3072]{1,0:T(8,128)} %get-tuple-element.90) | copy-start | bytes 4718596
  619.7 31.0 %copy-start.1 = (f32[128,3072]{1,0:T(8,128)S(1)}, f32[128,3072]{1,0:T(8,128)}, u32[]{:S(2)}) copy-start(f32[128,3072]{1,0:T(8,128)} %copy-done) | copy-start | bytes 4718596
  681.3 29.8 %copy-start.8 = (f32[128,3072]{1,0:T(8,128)S(1)}, f32[128,3072]{1,0:T(8,128)}, u32[]{:S(2)}) copy-start(f32[128,3072]{1,0:T(8,128)} %get-tuple-element.100) | copy-start | bytes 4718596
  741.7 33.7 %slice-start.6 = ((s8[6291456]{0:T(1024)(128)(4,1)}), s8[2097152]{0:T(1024)(128)(4,1)S(1)}, s32[]{:S(2)}) async-start(s8[6291456]{0:T(1024)(128)(4,1)} %bitcast.158), calls=%async_computation.6 | async-start | bytes 4194304
  771.8 4.1 slice-start.7
  775.3 5.6 copy-start.19
  811.4 39.8 %copy-start.11 = (f32[128,3072]{1,0:T(8,128)S(1)}, f32[128,3072]{1,0:T(8,128)}, u32[]{:S(2)}) copy-start(f32[128,3072]{1,0:T(8,128)} %get-tuple-element.130) | copy-start | bytes 4718596
  851.2 31.0 %copy-start.6 = (f32[128,3072]{1,0:T(8,128)S(1)}, f32[128,3072]{1,0:T(8,128)}, u32[]{:S(2)}) copy-start(f32[128,3072]{1,0:T(8,128)} %get-tuple-element.90) | copy-start | bytes 4718596
  882.2 30.8 %copy-start.2 = (f32[128,3072]{1,0:T(8,128)S(1)}, f32[128,3072]{1,0:T(8,128)}, u32[]{:S(2)}) copy-start(f32[128,3072]{1,0:T(8,128)} %copy-done) | copy-start | bytes 4718596
  973.0 30.8 %copy-start.14 = (f32[128,3072]{1,0:T(8,128)S(1)}, f32[128,3072]{1,0:T(8,128)}, u32[]{:S(2)}) copy-start(f32[128,3072]{1,0:T(8,128)} %copy-done.13) | copy-start | bytes 4718596
  973.0 30.8 %copy-start.18 = (f32[128,3072]{1,0:T(8,128)S(1)}, f32[128,3072]{1,0:T(8,128)}, u32[]{:S(2)}) copy-start(f32[128,3072]{1,0:T(8,128)} %get-tuple-element.74) | copy-start | bytes 4718596
where the time goes:
time: 1020 us; the launch traced here: 1010 us
  blocking collectives  730 us (72%)
  matrix products  102 us (10%)
  other arithmetic  97.6 us (10%)
  between operations  74.4 us (7%)
    psum x19, blocking collectives, global_dot(): return lax.psum(pair_dot_local(first, second), 'feat')  459 us
    psum x6, blocking collectives, local_solve(): logits = lax.psum(part_logits, 'feat')  150 us
    psum x5, blocking collectives, local_solve(): lax.psum(jnp.stack([pair_dot_local(y_vec, s_vec), pair_dot_local(y_vec, y...  121 us
    reduce_sum x38, other arithmetic, pair_dot_local(): return jnp.sum(first[0] * second[0]) + jnp.sum(first[1] * second[1])  78.7 us
    dot_general x6, matrix products, local_solve(): lax.dot_general(d_pre, x_f32, (((0,), (0,)), ((), ())), precision=FULL_PREC)  56.5 us
    dot_general x6, matrix products, local_solve(): lax.dot_general(x_f32, params[0], (((1,), (1,)), ((), ())), precision=FUL...  36.5 us

commit v1 on v0

v1 whole, which is shorter than its diff:
```python
import functools
import math

import jax
import jax.numpy as jnp
from jax import lax
from jax.experimental import pallas as pl
from jax.experimental.pallas import tpu as pltpu
from jax.sharding import PartitionSpec as P

NUM_ITERS = 6
HIST = 3
LANES = 128
SUBL = 8
ROW_CHUNK = 512
COL_CHUNK = 512
NUM_DOTS = 8
MESH = pl.DeviceIdType.MESH
F32 = jnp.float32
BF16 = jnp.bfloat16


def split3(val):
    high = val.astype(BF16)
    rest = val - high.astype(F32)
    mid = rest.astype(BF16)
    low = (rest - mid.astype(F32)).astype(BF16)
    return high, mid, low


def fold(val):
    rows, cols = val.shape
    part = jnp.sum(val.reshape(rows // SUBL, SUBL, cols), axis=0)
    total = part[:, :LANES]
    for start in range(LANES, cols, LANES):
        total = total + part[:, start : start + LANES]
    return total


def merge3(prod, rows):
    return (prod[2 * rows :] + prod[rows : 2 * rows]) + prod[:rows]


def kernel(
    axis, n, in_scale, out_scale,
    x_hbm, t_ref, win_hbm, wout_ref, reg_ref, step_ref,
    out_w, out_w2, out_loss,
    x_v, theta, grad, hist_s, hist_y, pre, hid, fac, q_s, q_y, q_g,
    split_d, split_g, resid, logits_v, coef,
    z_src, z_buf, d_src, d_buf,
    load_sem, out_sem, send_sem, recv_sem,
):
    num_rows, dim = x_v.shape
    hid_rows = grad.shape[0]
    row_tiles = num_rows // LANES
    me = lax.axis_index(axis)
    offsets = sorted(range(1, n), key=lambda off: -min(off, n - off))
    peers = [lax.rem(me + off, n) for off in offsets]

    barrier = pltpu.get_barrier_semaphore()
    for peer in peers:
        pl.semaphore_signal(barrier, inc=1, device_id={axis: peer}, device_id_type=MESH)

    w_load = pltpu.make_async_copy(win_hbm, theta.at[:, pl.ds(0, dim)], load_sem.at[0])
    w_load.start()
    x_loads = []
    for idx in range(num_rows // ROW_CHUNK):
        part = pl.ds(idx * ROW_CHUNK, ROW_CHUNK)
        load = pltpu.make_async_copy(x_hbm.at[part], x_v.at[part], load_sem.at[1 + idx])
        load.start()
        x_loads.append(load)

    reg = reg_ref[0]
    step = step_ref[0]
    lane = lax.broadcasted_iota(jnp.int32, (hid_rows, LANES), 1)
    eye = lane == lax.broadcasted_iota(jnp.int32, (hid_rows, LANES), 0)
    col_parts = [pl.ds(start, COL_CHUNK) for start in range(0, dim, COL_CHUNK)]
    tail = pl.ds(dim, LANES)

    def send_all(src, dst, sem):
        for peer in peers:
            pltpu.make_async_remote_copy(
                src_ref=src, dst_ref=dst.at[me], send_sem=send_sem.at[sem], recv_sem=recv_sem.at[sem],
                device_id={axis: peer}, device_id_type=MESH,
            ).start()

    def wait_all(dst, sem):
        others = dst.at[pl.ds(0, n - 1)]
        pltpu.make_async_copy(others, others, recv_sem.at[sem]).wait()
        pltpu.make_async_copy(others, others, send_sem.at[sem]).wait()

    def times_x(out_fn):
        for idx in range(num_rows // ROW_CHUNK):
            part = pl.ds(idx * ROW_CHUNK, ROW_CHUNK)
            prod = lax.dot_general(split_g[...], x_v[part, :], (((1,), (1,)), ((), ())), preferred_element_type=F32)
            out_fn(part, merge3(prod, hid_rows) * in_scale)

    def store_split(ref, part, val):
        for idx, term in enumerate(split3(val)):
            ref[idx * hid_rows : (idx + 1) * hid_rows, part] = term

    def send_logits(buf, sem):
        w2 = jnp.broadcast_to(theta[:, dim : dim + 1], (hid_rows, LANES))
        rows = []
        for idx in range(row_tiles):
            part = pl.ds(idx * LANES, LANES)
            act = jnp.tanh(pre[:, part])
            hid[:, part] = act
            rows.append(jnp.sum(fold(act * w2), axis=0, keepdims=True))
        z_mine = jnp.concatenate(rows, axis=0)
        z_src[...] = z_mine
        buf[me] = z_mine
        send_all(z_src, buf, sem)
        w2s = w2 * (out_scale * in_scale)
        for idx in range(row_tiles):
            part = pl.ds(idx * LANES, LANES)
            act = hid[:, part]
            fac[:, part] = w2s * (1.0 - act * act)

    def residual(buf, sem):
        wait_all(buf, sem)
        logits = jnp.sum(buf[...], axis=0) * out_scale
        logits_v[...] = logits
        resid[...] = (jax.nn.sigmoid(logits) - t_ref[...]) * (1.0 / num_rows)
        for idx in range(row_tiles):
            part = pl.ds(idx * LANES, LANES)
            store_split(split_d, part, fac[:, part] * resid[idx : idx + 1, :])

    def grad_tail():
        total = hid[:, :LANES] * resid[0:1, :]
        for idx in range(1, row_tiles):
            total = total + hid[:, idx * LANES : (idx + 1) * LANES] * resid[idx : idx + 1, :]
        g_out = jnp.sum(total, axis=1, keepdims=True) * out_scale
        return jnp.where(lane == 0, g_out, 0.0) + reg * theta[:, tail]

    def grad_part(part):
        prod = jnp.dot(split_d[...], x_v[:, part], preferred_element_type=F32)
        return merge3(prod, hid_rows) + reg * theta[:, part]

    def store_loss(idx):
        logits = logits_v[...]
        soft = jnp.maximum(logits, 0.0) + jnp.log1p(jnp.exp(-jnp.abs(logits)))
        out_loss[idx] = jnp.sum(soft - t_ref[...] * logits) * (1.0 / num_rows)

    def combine(cfs, slots, vec_g, vec_s, vec_y, part):
        rows, cols = vec_g.shape[0], part.size

        def scaled(cf, val):
            parts = [
                (val[:, start : start + LANES].reshape(rows // SUBL, SUBL, LANES) * cf[None]).reshape(rows, LANES)
                for start in range(0, cols, LANES)
            ]
            return parts[0] if len(parts) == 1 else jnp.concatenate(parts, axis=1)

        total = scaled(cfs[0], vec_g[:, part])
        for idx, slot in enumerate(slots):
            total = total + scaled(cfs[1 + idx], vec_s[slot, :, part])
            total = total + scaled(cfs[1 + HIST + idx], vec_y[slot, :, part])
        return total

    def move(k, cfs, slots):
        slot_new = slots[-1]
        s_part = combine(cfs, slots, grad, hist_s, hist_y, tail)
        hist_s[slot_new, :, tail] = s_part
        theta[:, tail] = theta[:, tail] + s_part
        for idx in range(row_tiles):
            part = pl.ds(idx * LANES, LANES)
            q_part = combine(cfs, slots, q_g, q_s, q_y, part)
            q_s[slot_new, :, part] = q_part
            pre[:, part] = pre[:, part] + q_part

    def move_rest(cfs, slots):
        slot_new = slots[-1]
        acc = fold(grad[:, tail] * hist_s[slot_new, :, tail])
        for part in col_parts:
            s_part = combine(cfs, slots, grad, hist_s, hist_y, part)
            hist_s[slot_new, :, part] = s_part
            theta[:, part] = theta[:, part] + s_part
            acc = acc + fold(grad[:, part] * s_part)
        return acc

    def new_grad(slots, acc_gs):
        new, old1, old2 = slots
        accs = [None] * 7

        def add(part, g_new):
            g_old = grad[:, part]
            y_new = g_new - g_old
            grad[:, part] = g_new
            others = [
                hist_s[new, :, part], hist_s[old1, :, part], hist_s[old2, :, part],
                y_new, hist_y[old1, :, part], hist_y[old2, :, part], g_old,
            ]
            hist_y[new, :, part] = y_new
            for idx, other in enumerate(others):
                term = fold(y_new * other)
                accs[idx] = term if accs[idx] is None else accs[idx] + term

        add(tail, grad_tail())
        for part in col_parts:
            add(part, grad_part(part))
        sums = [jnp.sum(acc, axis=0, keepdims=True) for acc in accs + [acc_gs]]
        totals = jnp.sum(jnp.concatenate(sums, axis=0), axis=1, keepdims=True)
        packed = jnp.sum(jnp.where(eye[:NUM_DOTS], totals, 0.0), axis=0, keepdims=True)
        d_src[...] = packed
        d_buf[me] = packed
        send_all(d_src, d_buf, 2)

    def new_q(slot):
        for part in col_parts:
            store_split(split_g, part, grad[:, part])

        def keep(part, val):
            q_y[slot, :, part] = val - q_g[:, part]
            q_g[:, part] = val

        times_x(keep)

    def two_loop(carry):
        rho1, rho2, psg0, psg1, pyg0, pyg1, pys1, yy11, yy12, yy22 = carry
        wait_all(d_buf, 2)
        total = jnp.sum(d_buf[...], axis=0)
        ys0, ys1, ys2, yy0, yy1, yy2, ygp, gs0 = (
            jnp.broadcast_to(total[:, idx : idx + 1], (SUBL, LANES)) for idx in range(NUM_DOTS)
        )
        sg0, sg1, sg2 = gs0 + ys0, psg0 + ys1, psg1 + ys2
        yg0, yg1, yg2 = ygp + yy0, pyg0 + yy1, pyg1 + yy2
        rho0 = 1.0 / ys0
        gamma = ys0 / yy0
        a0 = rho0 * sg0
        a1 = rho1 * (sg1 - a0 * ys1)
        a2 = rho2 * (sg2 - a0 * ys2 - a1 * pys1)
        yq2 = yg2 - a0 * yy2 - a1 * yy12 - a2 * yy22
        yq1 = yg1 - a0 * yy1 - a1 * yy11 - a2 * yy12
        yq0 = yg0 - a0 * yy0 - a1 * yy1 - a2 * yy2
        c2 = a2 - rho2 * (gamma * yq2)
        c1 = a1 - rho1 * (gamma * yq1 + c2 * pys1)
        c0 = a0 - rho0 * (gamma * yq0 + c2 * ys2 + c1 * ys1)
        sgam = step * gamma
        for idx, val in enumerate((-sgam, -step * c0, -step * c1, -step * c2, sgam * a0, sgam * a1, sgam * a2)):
            coef[idx] = val
        return rho0, rho1, sg0, sg1, yg0, yg1, ys1, yy0, yy1, yy11

    def load_coef():
        return [coef[idx] for idx in range(1 + 2 * HIST)]

    w2_row = jnp.broadcast_to(wout_ref[...], (hid_rows, LANES))
    w2_col = jnp.sum(jnp.where(eye, w2_row, 0.0), axis=1, keepdims=True)
    theta[:, tail] = jnp.where(lane == 0, w2_col, 0.0)
    w_load.wait()
    for part in col_parts:
        store_split(split_g, part, theta[:, part])
    for idx in range(num_rows // ROW_CHUNK):
        part = pl.ds(idx * ROW_CHUNK, ROW_CHUNK)
        x_loads[idx].wait()
        prod = lax.dot_general(split_g[...], x_v[part, :], (((1,), (1,)), ((), ())), preferred_element_type=F32)
        pre[:, part] = merge3(prod, hid_rows) * in_scale
    pl.semaphore_wait(barrier, n - 1)
    send_logits(z_buf.at[0], 0)
    hist_s[...] = jnp.zeros_like(hist_s)
    hist_y[...] = jnp.zeros_like(hist_y)
    q_s[...] = jnp.zeros_like(q_s)
    q_y[...] = jnp.zeros_like(q_y)
    residual(z_buf.at[0], 0)
    grad[:, tail] = grad_tail()
    for part in col_parts:
        g_part = grad_part(part)
        grad[:, part] = g_part
        store_split(split_g, part, g_part)

    def keep_first(part, val):
        q_g[:, part] = val

    times_x(keep_first)
    store_loss(0)
    coef[...] = jnp.zeros_like(coef)
    coef[0] = jnp.full((SUBL, LANES), -step, F32)

    def slots_at(k):
        return lax.rem(k, HIST), lax.rem(k + 2, HIST), lax.rem(k + 1, HIST)

    def head(k):
        new, old1, old2 = slots_at(k)
        prev = (old1, old2, new)
        cfs = load_coef()
        move(k, cfs, prev)
        send_logits(z_buf.at[1], 1)
        acc_gs = move_rest(cfs, prev)
        residual(z_buf.at[1], 1)
        new_grad((new, old1, old2), acc_gs)
        return new

    def body(k, carry):
        new = head(k)
        new_q(new)
        store_loss(k)
        return two_loop(carry)

    zero = jnp.zeros((SUBL, LANES), F32)
    carry = lax.fori_loop(1, NUM_ITERS - 1, body, (zero,) * 10)

    last = NUM_ITERS - 1
    head(last)
    store_loss(last)
    two_loop(carry)
    new, old1, old2 = (last % HIST, (last + 2) % HIST, (last + 1) % HIST)
    cfs = load_coef()
    slots = (new, old1, old2)
    w2_new = theta[:, tail] + combine(cfs, slots, grad, hist_s, hist_y, tail)
    w2_new = jnp.broadcast_to(w2_new[:, 0:1], (hid_rows, LANES))
    out_w2[...] = jnp.sum(jnp.where(eye, w2_new, 0.0), axis=0, keepdims=True)
    stores = []
    for idx, part in enumerate(col_parts):
        theta[:, part] = theta[:, part] + combine(cfs, slots, grad, hist_s, hist_y, part)
        store = pltpu.make_async_copy(theta.at[:, part], out_w.at[:, part], out_sem.at[idx])
        store.start()
        stores.append(store)
    for store in stores:
        store.wait()


def solution(mesh):
    n = mesh.shape["feat"]

    def local_solve(x_loc, t_loc, win_loc, wout_loc, reg_loc, step_loc):
        num_rows, dim = x_loc.shape
        hid_rows = win_loc.shape[0]
        wide = dim + LANES
        in_scale = 1.0 / math.sqrt(dim)
        out_scale = 1.0 / math.sqrt(hid_rows * n)
        row_tiles = num_rows // LANES
        vmem = pl.BlockSpec(memory_space=pltpu.VMEM)
        smem = pl.BlockSpec(memory_space=pltpu.SMEM)
        anym = pl.BlockSpec(memory_space=pl.ANY)
        new_w, new_w2, losses = pl.pallas_call(
            functools.partial(kernel, "feat", n, in_scale, out_scale),
            out_shape=(
                jax.ShapeDtypeStruct((hid_rows, dim), F32),
                jax.ShapeDtypeStruct((1, hid_rows), F32),
                jax.ShapeDtypeStruct((NUM_ITERS,), F32),
            ),
            in_specs=[anym, vmem, anym, vmem, smem, smem],
            out_specs=(anym, vmem, smem),
            scratch_shapes=[
                pltpu.VMEM((num_rows, dim), BF16),
                pltpu.VMEM((hid_rows, wide), F32),
                pltpu.VMEM((hid_rows, wide), F32),
                pltpu.VMEM((HIST, hid_rows, wide), F32),
                pltpu.VMEM((HIST, hid_rows, wide), F32),
                pltpu.VMEM((hid_rows, num_rows), F32),
                pltpu.VMEM((hid_rows, num_rows), F32),
                pltpu.VMEM((hid_rows, num_rows), F32),
                pltpu.VMEM((HIST, hid_rows, num_rows), F32),
                pltpu.VMEM((HIST, hid_rows, num_rows), F32),
                pltpu.VMEM((hid_rows, num_rows), F32),
                pltpu.VMEM((3 * hid_rows, num_rows), BF16),
                pltpu.VMEM((3 * hid_rows, dim), BF16),
                pltpu.VMEM((row_tiles, LANES), F32),
                pltpu.VMEM((row_tiles, LANES), F32),
                pltpu.VMEM((1 + 2 * HIST, SUBL, LANES), F32),
                pltpu.VMEM((row_tiles, LANES), F32),
                pltpu.VMEM((2, n, row_tiles, LANES), F32),
                pltpu.VMEM((1, LANES), F32),
                pltpu.VMEM((n, 1, LANES), F32),
                pltpu.SemaphoreType.DMA((1 + num_rows // ROW_CHUNK,)),
                pltpu.SemaphoreType.DMA((dim // COL_CHUNK,)),
                pltpu.SemaphoreType.DMA((3,)),
                pltpu.SemaphoreType.DMA((3,)),
            ],
            compiler_params=pltpu.CompilerParams(
                collective_id=0, has_side_effects=True, vmem_limit_bytes=60 * 1024 * 1024
            ),
        )(x_loc, t_loc.reshape(row_tiles, LANES), win_loc, wout_loc.reshape(1, hid_rows), reg_loc, step_loc)
        return new_w, new_w2.reshape(hid_rows), losses

    specs_in = (P("prob", None), P("prob"), P(("prob", "feat"), None), P(("prob", "feat")), P("prob"), P("prob"))
    specs_out = (P(("prob", "feat"), None), P(("prob", "feat")), P("prob"))
    return jax.shard_map(local_solve, mesh=mesh, in_specs=specs_in, out_specs=specs_out, check_vma=False)
```

time: 1020 us -> 98.6 us (0.10); the launches traced: 1010 us -> 98.5 us
  blocking collectives: 730 us -> 0 us
  matrix products: 102 us -> 0 us
  other arithmetic: 97.6 us -> 0 us
  Pallas kernels: 0 us -> 92.8 us
  between operations: 74.4 us -> 1.95 us
    psum x30 -> x0, blocking collectives: 730 us -> none  [the longest x19 459 us: global_dot(): return lax.psum(pair_dot_local(first, second), 'feat')]
    dot_general x24 -> x0, matrix products: 102 us -> none  [the longest x6 56.5 us: local_solve(): lax.dot_general(d_pre, x_f32, (((0,), (0,)), ((), ())), precision=FULL_PREC)]
    pallas_call x0 -> x1, Pallas kernels: none -> 92.8 us  [local_solve(): pl.pallas_call(functools.partial(kernel, 'feat', n, in_scale, out_scale),...]
    reduce_sum x39 -> x0, other arithmetic: 79.4 us -> none  [the longest x38 78.7 us: pair_dot_local(): return jnp.sum(first[0] * second[0]) + jnp.sum(first[1] * second[1])]
    add x6 -> x0, other arithmetic: 17.7 us -> none  [pair_axpy(): return (base[0] + coef * other[0], base[1] + coef * other[1])]
where the time goes in v1:
time: 98.6 us; the launch traced here: 98.5 us
  Pallas kernels  92.8 us (94%)
  local copies, waits for them, and re-layouts  3.73 us (4%)
  between operations  1.95 us (2%)
    pallas_call x1, Pallas kernels, local_solve(): pl.pallas_call(functools.partial(kernel, 'feat', n, in_scale, out_scale),...  92.8 us
    unnamed x7, local copies, waits for them, and re-layouts  3.73 us

profile of v1, /device:TPU:21, one launch (start us, length us, event | category | flops | bytes accessed | tf_op | source)
XLA Modules:
  0.0 98.5 jit_solution(1039056512344335591)
XLA Ops:
  1.9 92.8 %shard_map.85 = (f32[128,3072]{1,0:T(8,128)}, f32[1,128]{1,0:T(1,128)}, f32[6]{0:T(128)}) custom-call(bf16[1024,3072]{1,0:T(8,128)(2,1)} %x_hbm.1, f32[8,128]{1,0:T(8,128)} %bitcast.3, f32[128,3072]{1,0:T(8,128)} %win_hbm.1, f32[1,128]{1,0:T(1,128)} %bitcast.4, f32[1]{0:T(128)S(6)} %copy.12.reg_ref, f32[1]{0:T(128)S(6)} %copy.13.step_ref), custom_call_target="tpu_custom_call" | custom-call | tf_op jit(solution)/shard_map/pallas_call | solution.py:335
  94.7 0.0 copy-start.1
  94.7 0.0 copy-start
  94.7 2.7 %copy.14 = f32[128,3072]{1,0:T(8,128)} copy(f32[128,3072]{1,0:T(8,128)} %get-tuple-element.12) | data formatting | bytes 3145728
  97.4 0.0 copy-done.1
  97.4 0.5 copy.15
  98.0 0.0 copy-done
  98.0 0.5 copy.16
Async XLA Ops:
  94.7 2.7 %copy-start.1 = (f32[1,128]{1,0:T(1,128)S(1)}, f32[1,128]{1,0:T(1,128)}, u32[]{:S(2)}) copy-start(f32[1,128]{1,0:T(1,128)} %get-tuple-element.7) | copy-start | bytes 1540
  94.7 3.2 %copy-start = (f32[6]{0:T(128)S(1)}, f32[6]{0:T(128)}, u32[]{:S(2)}) copy-start(f32[6]{0:T(128)} %get-tuple-element.14) | copy-start | bytes 76

commit v2 on v1

--- a/solution.py
+++ b/solution.py
@@ -43,12 +43,13 @@
 
 def kernel(
     axis, n, in_scale, out_scale,
-    x_hbm, t_ref, win_hbm, wout_ref, reg_ref, step_ref,
+    x_hbm, t_hbm, win_hbm, wout_hbm, reg_hbm, step_hbm,
     out_w, out_w2, out_loss,
+    t_ref, wout_ref, reg_ref, step_ref,
     x_v, theta, grad, hist_s, hist_y, pre, hid, fac, q_s, q_y, q_g,
     split_d, split_g, resid, logits_v, coef,
     z_src, z_buf, d_src, d_buf,
-    load_sem, out_sem, send_sem, recv_sem,
+    load_sem, small_sem, send_sem, recv_sem,
 ):
     num_rows, dim = x_v.shape
     hid_rows = grad.shape[0]
@@ -56,10 +57,6 @@
     me = lax.axis_index(axis)
     offsets = sorted(range(1, n), key=lambda off: -min(off, n - off))
     peers = [lax.rem(me + off, n) for off in offsets]
-
-    barrier = pltpu.get_barrier_semaphore()
-    for peer in peers:
-        pl.semaphore_signal(barrier, inc=1, device_id={axis: peer}, device_id_type=MESH)
 
     w_load = pltpu.make_async_copy(win_hbm, theta.at[:, pl.ds(0, dim)], load_sem.at[0])
     w_load.start()
@@ -70,6 +67,18 @@
         load.start()
         x_loads.append(load)
 
+    smalls = []
+    for idx, (src, dst) in enumerate(((t_hbm, t_ref), (wout_hbm, wout_ref), (reg_hbm, reg_ref), (step_hbm, step_ref))):
+        load = pltpu.make_async_copy(src, dst, small_sem.at[idx])
+        load.start()
+        smalls.append(load)
+
+    barrier = pltpu.get_barrier_semaphore()
+    for peer in peers:
+        pl.semaphore_signal(barrier, inc=1, device_id={axis: peer}, device_id_type=MESH)
+
+    for load in smalls:
+        load.wait()
     reg = reg_ref[0]
     step = step_ref[0]
     lane = lax.broadcasted_iota(jnp.int32, (hid_rows, LANES), 1)
@@ -309,14 +318,19 @@
     w2_new = theta[:, tail] + combine(cfs, slots, grad, hist_s, hist_y, tail)
     w2_new = jnp.broadcast_to(w2_new[:, 0:1], (hid_rows, LANES))
     out_w2[...] = jnp.sum(jnp.where(eye, w2_new, 0.0), axis=0, keepdims=True)
-    stores = []
-    for idx, part in enumerate(col_parts):
-        theta[:, part] = theta[:, part] + combine(cfs, slots, grad, hist_s, hist_y, part)
-        store = pltpu.make_async_copy(theta.at[:, part], out_w.at[:, part], out_sem.at[idx])
-        store.start()
-        stores.append(store)
-    for store in stores:
-        store.wait()
+    for part in col_parts:
+        out_w[:, part] = theta[:, part] + combine(cfs, slots, grad, hist_s, hist_y, part)
+
+
+def write_out(w_ref, w2_ref, loss_ref, out_w, out_w2, out_loss, sems):
+    copies = [
+        pltpu.make_async_copy(src, dst, sems.at[idx])
+        for idx, (src, dst) in enumerate(((w_ref, out_w), (w2_ref, out_w2), (loss_ref, out_loss)))
+    ]
+    for copy in copies:
+        copy.start()
+    for copy in copies:
+        copy.wait()
 
 
 def solution(mesh):
@@ -332,16 +346,17 @@
         vmem = pl.BlockSpec(memory_space=pltpu.VMEM)
         smem = pl.BlockSpec(memory_space=pltpu.SMEM)
         anym = pl.BlockSpec(memory_space=pl.ANY)
-        new_w, new_w2, losses = pl.pallas_call(
+        shapes = ((hid_rows, dim), (1, hid_rows), (NUM_ITERS,))
+        solved = pl.pallas_call(
             functools.partial(kernel, "feat", n, in_scale, out_scale),
-            out_shape=(
-                jax.ShapeDtypeStruct((hid_rows, dim), F32),
-                jax.ShapeDtypeStruct((1, hid_rows), F32),
-                jax.ShapeDtypeStruct((NUM_ITERS,), F32),
-            ),
-            in_specs=[anym, vmem, anym, vmem, smem, smem],
-            out_specs=(anym, vmem, smem),
+            out_shape=(pltpu.VMEM(shapes[0], F32), pltpu.VMEM(shapes[1], F32), pltpu.SMEM(shapes[2], F32)),
+            in_specs=[anym] * 6,
+            out_specs=(vmem, vmem, smem),
             scratch_shapes=[
+                pltpu.VMEM((row_tiles, LANES), F32),
+                pltpu.VMEM((1, hid_rows), F32),
+                pltpu.SMEM((1,), F32),
+                pltpu.SMEM((1,), F32),
                 pltpu.VMEM((num_rows, dim), BF16),
                 pltpu.VMEM((hid_rows, wide), F32),
                 pltpu.VMEM((hid_rows, wide), F32),
@@ -363,14 +378,28 @@
                 pltpu.VMEM((1, LANES), F32),
                 pltpu.VMEM((n, 1, LANES), F32),
                 pltpu.SemaphoreType.DMA((1 + num_rows // ROW_CHUNK,)),
-                pltpu.SemaphoreType.DMA((dim // COL_CHUNK,)),
+                pltpu.SemaphoreType.DMA((4,)),
                 pltpu.SemaphoreType.DMA((3,)),
                 pltpu.SemaphoreType.DMA((3,)),
             ],
             compiler_params=pltpu.CompilerParams(
-                collective_id=0, has_side_effects=True, vmem_limit_bytes=60 * 1024 * 1024
+                collective_id=0, has_side_effects=True, vmem_limit_bytes=61 * 1024 * 1024
             ),
-        )(x_loc, t_loc.reshape(row_tiles, LANES), win_loc, wout_loc.reshape(1, hid_rows), reg_loc, step_loc)
+        )(
+            *(
+                pltpu.with_memory_space_constraint(arg, pltpu.HBM)
+                for arg in (x_loc, t_loc.reshape(row_tiles, LANES), win_loc, wout_loc.reshape(1, hid_rows))
+            ),
+            reg_loc, step_loc,
+        )
+        new_w, new_w2, losses = pl.pallas_call(
+            write_out,
+            out_shape=tuple(jax.ShapeDtypeStruct(shape, F32) for shape in shapes),
+            in_specs=[vmem, vmem, smem],
+            out_specs=(anym, anym, anym),
+            scratch_shapes=[pltpu.SemaphoreType.DMA((3,))],
+            compiler_params=pltpu.CompilerParams(vmem_limit_bytes=1024 * 1024),
+        )(*solved)
         return new_w, new_w2.reshape(hid_rows), losses
 
     specs_in = (P("prob", None), P("prob"), P(("prob", "feat"), None), P(("prob", "feat")), P("prob"), P("prob"))

time: 98.6 us -> 95.1 us (0.965)
  local copies, waits for them, and re-layouts: 3.73 us -> 0 us
    unnamed x7 -> x0, local copies, waits for them, and re-layouts: 3.73 us -> none
    pallas_call x0 -> x1, Pallas kernels: none -> 1.18 us  [local_solve(): pl.pallas_call(write_out, out_shape=tuple((jax.ShapeDtypeStruct(shape, F3...]
    pallas_call x1, Pallas kernels: 92.8 us -> 91.7 us  [local_solve(): pl.pallas_call(functools.partial(kernel, 'feat', n, in_scale, out_scale),...]
where the time goes in v2:
time: 95.1 us; the launch traced here: 95 us
  Pallas kernels  92.9 us (98%)
  between operations  2.11 us (2%)
    pallas_call x1, Pallas kernels, local_solve(): pl.pallas_call(functools.partial(kernel, 'feat', n, in_scale, out_scale),...  91.7 us

profile of v2, /device:TPU:21, one launch (start us, length us, event | category | flops | bytes accessed | tf_op | source)
XLA Modules:
  0.0 95.0 jit_solution(16728144579255193775)
XLA Ops:
  1.9 91.7 %shard_map.85 = (f32[128,3072]{1,0:T(8,128)S(1)}, f32[1,128]{1,0:T(1,128)S(1)}, f32[6]{0:T(128)S(4)}) custom-call(bf16[1024,3072]{1,0:T(8,128)(2,1)} %x_hbm.1, f32[8,128]{1,0:T(8,128)} %bitcast.3, f32[128,3072]{1,0:T(8,128)} %win_hbm.1, f32[1,128]{1,0:T(1,128)} %bitcast.4, f32[1]{0:T(128)S(6)} %copy.9.reg_hbm, f32[1]{0:T(128)S(6)} %copy.10.step_hbm), custom_call_target="tpu_custom_call" | custom-call | tf_op jit(solution)/shard_map/pallas_call | solution.py:350
  93.6 1.2 %shard_map.86 = (f32[128,3072]{1,0:T(8,128)}, f32[1,128]{1,0:T(1,128)}, f32[6]{0:T(128)}) custom-call(f32[128,3072]{1,0:T(8,128)S(1)} %get-tuple-element.9.w_ref, f32[1,128]{1,0:T(1,128)S(1)} %get-tuple-element.10.w2_ref, f32[6]{0:T(128)S(4)} %get-tuple-element.11.loss_ref), custom_call_target="tpu_custom_call" | custom-call | tf_op jit(solution)/shard_map/pallas_call | solution.py:395

commit v3 on v2

v3 whole, which is shorter than its diff:
```python
import functools
import math

import jax
import jax.numpy as jnp
from jax import lax
from jax.experimental import pallas as pl
from jax.experimental.pallas import tpu as pltpu
from jax.sharding import PartitionSpec as P

NUM_ITERS = 6
HIST = 3
LANES = 128
SUBL = 8
ROW_CHUNK = 512
COL_CHUNK = 512
NUM_DOTS = 8
MESH = pl.DeviceIdType.MESH
F32 = jnp.float32
BF16 = jnp.bfloat16


def split3(val):
    high = val.astype(BF16)
    rest = val - high.astype(F32)
    mid = rest.astype(BF16)
    low = (rest - mid.astype(F32)).astype(BF16)
    return high, mid, low


def fold(val):
    rows, cols = val.shape
    part = jnp.sum(val.reshape(rows // SUBL, SUBL, cols), axis=0)
    total = part[:, :LANES]
    for start in range(LANES, cols, LANES):
        total = total + part[:, start : start + LANES]
    return total


def merge3(prod, rows):
    return (prod[2 * rows :] + prod[rows : 2 * rows]) + prod[:rows]


def power_of_two(peak):
    scale = jnp.float32(1.0)
    inverse = jnp.float32(1.0)
    for up in (True, False):
        for bits in (64, 32, 16, 8, 4, 2):
            big, small = 2.0**bits, 2.0**-bits
            grow, shrink = (small, big) if up else (big, small)
            hit = (peak >= big) if up else (peak <= small)
            peak = jnp.where(hit, peak * grow, peak)
            inverse = jnp.where(hit, inverse * grow, inverse)
            scale = jnp.where(hit, scale * shrink, scale)
    return scale, inverse


def kernel(
    axis, n, in_scale, out_scale,
    x_hbm, t_hbm, win_hbm, wout_hbm, reg_hbm, step_hbm,
    out_w, out_w2, out_loss,
    t_ref, wout_ref, reg_ref, step_ref,
    x_v, xs, w0, gram, g_parts, pre, pre0, hid, fac, d_old,
    q_s, q_y, q_g, d_s, d_y, d_g, m_s, m_y, m_g, w2, cv,
    split_d, split_w, resid, logits_v, coef,
    z_src, z_buf, dot_src, dot_buf,
    load_sem, small_sem, send_sem, recv_sem,
):
    num_rows, dim = x_v.shape
    hid_rows = w0.shape[0]
    row_tiles = num_rows // LANES
    me = lax.axis_index(axis)
    offsets = sorted(range(1, n), key=lambda off: -min(off, n - off))
    peers = [lax.rem(me + off, n) for off in offsets]

    w_load = pltpu.make_async_copy(win_hbm, w0, load_sem.at[0])
    w_load.start()
    x_loads = []
    row_parts = [pl.ds(start, ROW_CHUNK) for start in range(0, num_rows, ROW_CHUNK)]
    for idx, part in enumerate(row_parts):
        load = pltpu.make_async_copy(x_hbm.at[part], x_v.at[part], load_sem.at[1 + idx])
        load.start()
        x_loads.append(load)
    smalls = []
    for idx, (src, dst) in enumerate(((t_hbm, t_ref), (wout_hbm, wout_ref), (reg_hbm, reg_ref), (step_hbm, step_ref))):
        load = pltpu.make_async_copy(src, dst, small_sem.at[idx])
        load.start()
        smalls.append(load)

    barrier = pltpu.get_barrier_semaphore()
    for peer in peers:
        pl.semaphore_signal(barrier, inc=1, device_id={axis: peer}, device_id_type=MESH)

    for load in smalls:
        load.wait()
    reg = reg_ref[0]
    step = step_ref[0]
    eye = lax.broadcasted_iota(jnp.int32, (hid_rows, LANES), 1) == lax.broadcasted_iota(jnp.int32, (hid_rows, LANES), 0)
    unit = lax.broadcasted_iota(jnp.int32, (SUBL, LANES), 0)
    col_parts = [pl.ds(start, COL_CHUNK) for start in range(0, dim, COL_CHUNK)]
    tiles = [pl.ds(start, LANES) for start in range(0, num_rows, LANES)]
    sums, cfrow, w2rows = pl.ds(0, SUBL), pl.ds(SUBL, SUBL), pl.ds(2 * SUBL, hid_rows)
    top = pl.ds(SUBL, 1)

    def send_all(src, dst, sem):
        for peer in peers:
            pltpu.make_async_remote_copy(
                src_ref=src, dst_ref=dst.at[me], send_sem=send_sem.at[sem], recv_sem=recv_sem.at[sem],
                device_id={axis: peer}, device_id_type=MESH,
            ).start()

    def wait_all(dst, sem):
        others = dst.at[pl.ds(0, n - 1)]
        pltpu.make_async_copy(others, others, recv_sem.at[sem]).wait()
        pltpu.make_async_copy(others, others, send_sem.at[sem]).wait()

    def splat(row):
        return jnp.broadcast_to(row, (SUBL, LANES))

    def store_split(ref, part, val):
        for idx, term in enumerate(split3(val)):
            ref[idx * hid_rows : (idx + 1) * hid_rows, part] = term

    def send_logits(buf, sem):
        rows = []
        for part in tiles:
            act = jnp.tanh(pre[:, part])
            hid[:, part] = act
            rows.append(jnp.sum(fold(act * w2[...]), axis=0, keepdims=True))
        z_mine = jnp.concatenate(rows, axis=0)
        z_src[...] = z_mine
        buf[me] = z_mine
        send_all(z_src, buf, sem)
        w2s = w2[...] * out_scale
        for part in tiles:
            act = hid[:, part]
            fac[:, part] = w2s * (1.0 - act * act)

    def residual(buf, sem):
        wait_all(buf, sem)
        logits = jnp.sum(buf[...], axis=0) * out_scale
        logits_v[...] = logits
        resid[...] = (jax.nn.sigmoid(logits) - t_ref[...]) * (1.0 / num_rows)

    def w2_grad():
        total = hid[:, tiles[0]] * resid[0:1, :]
        for idx in range(1, row_tiles):
            total = total + hid[:, tiles[idx]] * resid[idx : idx + 1, :]
        g_out = jnp.sum(total, axis=1, keepdims=True) * out_scale
        return jnp.broadcast_to(g_out, (hid_rows, LANES)) + reg * w2[...]

    def gram_times(part):
        high = jnp.dot(split_d[...], gram[0, :, part], preferred_element_type=F32)
        mid = jnp.dot(split_d[: 2 * hid_rows], gram[1, :, part], preferred_element_type=F32)
        low = jnp.dot(split_d[:hid_rows], gram[2, :, part], preferred_element_type=F32)
        small = (high[2 * hid_rows :] + mid[hid_rows:]) + low
        return (((high[hid_rows : 2 * hid_rows] + mid[:hid_rows]) + small + high[:hid_rows]) * x_scale) * x_scale

    def keep_g_part(idx):
        for part in col_parts:
            prod = jnp.dot(split_d[...], xs[:, part], preferred_element_type=F32)
            g_parts[idx, :, part] = merge3(prod, hid_rows) * in_scale * x_scale

    def store_loss(idx):
        logits = logits_v[...]
        soft = jnp.maximum(logits, 0.0) + jnp.log1p(jnp.exp(-jnp.abs(logits)))
        out_loss[idx] = jnp.sum(soft - t_ref[...] * logits) * (1.0 / num_rows)

    def combine(cfs, slots, vec_g, vec_s, vec_y, rows, part):
        def scaled(cf, val):
            count = val.shape[0]
            return (val.reshape(count // SUBL, SUBL, LANES) * cf[None]).reshape(count, LANES)

        total = scaled(cfs[0], vec_g[rows, part])
        for idx, slot in enumerate(slots):
            total = total + scaled(cfs[1 + idx], vec_s[slot, rows, part])
            total = total + scaled(cfs[1 + HIST + idx], vec_y[slot, rows, part])
        return total

    every, lanes = pl.ds(0, hid_rows), pl.ds(0, LANES)

    def move(cfs, slots):
        new = slots[-1]
        s_part = combine(cfs, slots, m_g, m_s, m_y, w2rows, lanes)
        m_s[new, w2rows, :] = s_part
        w2[...] = w2[...] + s_part
        for part in tiles:
            q_part = combine(cfs, slots, q_g, q_s, q_y, every, part)
            q_s[new, :, part] = q_part
            pre[:, part] = pre[:, part] + q_part

    def move_rest(cfs, slots):
        new = slots[-1]
        s_part = combine(cfs, slots, m_g, m_s, m_y, pl.ds(0, 2 * SUBL), lanes)
        m_s[new, pl.ds(0, 2 * SUBL), :] = s_part
        cv[...] = cv[...] + s_part[SUBL:]
        acc = splat(m_g[top, :]) * s_part[:SUBL] + fold(m_g[w2rows, :] * m_s[new, w2rows, :]) * (1.0 / LANES)
        for part in tiles:
            d_part = combine(cfs, slots, d_g, d_s, d_y, every, part)
            d_s[new, :, part] = d_part
            acc = acc + fold(d_g[:, part] * q_s[new, :, part])
        return acc

    def new_grad(k, slots, acc_gs):
        new, old1, old2 = slots
        w2_part = w2_grad() - m_g[w2rows, :]
        acc_w0 = jnp.zeros((SUBL, LANES), F32)
        for idx, part in enumerate(tiles):
            d_new = fac[:, part] * resid[idx : idx + 1, :]
            diff = d_new - d_old[:, part]
            d_old[:, part] = d_new
            store_split(split_d, part, diff)
            d_y[new, :, part] = reg * d_s[new, :, part] + diff
            acc_w0 = acc_w0 + fold(diff * pre0[:, part])
        w0_y = reg * m_s[new, sums, :] + acc_w0
        cf_y = reg * m_s[new, cfrow, :] + jnp.where(unit == k + 1, 1.0, 0.0)
        c_y = splat(cf_y[0:1, :])
        m_y[new, sums, :] = w0_y
        m_y[new, cfrow, :] = cf_y
        m_y[new, w2rows, :] = w2_part
        others = [(q_s, m_s, new), (q_s, m_s, old1), (q_s, m_s, old2), (q_y, m_y, old1), (q_y, m_y, old2)]
        accs = [
            c_y * m[slot, sums, :] + fold(w2_part * m[slot, w2rows, :]) * (1.0 / LANES) for _, m, slot in others
        ]
        acc_gp = c_y * m_g[sums, :] + fold(w2_part * m_g[w2rows, :]) * (1.0 / LANES)
        acc_yy = c_y * w0_y + fold(w2_part * w2_part) * (1.0 / LANES)
        for part in row_parts:
            d_part = d_y[new, :, part]
            for idx, (q, _, slot) in enumerate(others):
                accs[idx] = accs[idx] + fold(d_part * q[slot, :, part])
            q_old = q_g[:, part]
            acc_gp = acc_gp + fold(d_part * q_old)
            q_new = reg * q_s[new, :, part] + gram_times(part)
            q_y[new, :, part] = q_new
            q_g[:, part] = q_old + q_new
            acc_yy = acc_yy + fold(d_part * q_new)
        order = accs[:3] + [acc_yy] + accs[3:] + [acc_gp, acc_gs]
        rows = [jnp.sum(acc, axis=0, keepdims=True) for acc in order]
        totals = jnp.sum(jnp.concatenate(rows, axis=0), axis=1, keepdims=True)
        packed = jnp.sum(jnp.where(eye[:NUM_DOTS], totals, 0.0), axis=0, keepdims=True)
        dot_src[...] = packed
        dot_buf[me] = packed
        send_all(dot_src, dot_buf, 2)
        m_g[...] = m_g[...] + m_y[new]
        for part in tiles:
            d_g[:, part] = d_g[:, part] + d_y[new, :, part]

    def two_loop(carry):
        rho1, rho2, psg0, psg1, pyg0, pyg1, pys1, yy11, yy12, yy22 = carry
        wait_all(dot_buf, 2)
        total = jnp.sum(dot_buf[...], axis=0)
        ys0, ys1, ys2, yy0, yy1, yy2, ygp, gs0 = (
            jnp.broadcast_to(total[:, idx : idx + 1], (SUBL, LANES)) for idx in range(NUM_DOTS)
        )
        sg0, sg1, sg2 = gs0 + ys0, psg0 + ys1, psg1 + ys2
        yg0, yg1, yg2 = ygp + yy0, pyg0 + yy1, pyg1 + yy2
        rho0 = 1.0 / ys0
        gamma = ys0 / yy0
        a0 = rho0 * sg0
        a1 = rho1 * (sg1 - a0 * ys1)
        a2 = rho2 * (sg2 - a0 * ys2 - a1 * pys1)
        yq2 = yg2 - a0 * yy2 - a1 * yy12 - a2 * yy22
        yq1 = yg1 - a0 * yy1 - a1 * yy11 - a2 * yy12
        yq0 = yg0 - a0 * yy0 - a1 * yy1 - a2 * yy2
        c2 = a2 - rho2 * (gamma * yq2)
        c1 = a1 - rho1 * (gamma * yq1 + c2 * pys1)
        c0 = a0 - rho0 * (gamma * yq0 + c2 * ys2 + c1 * ys1)
        sgam = step * gamma
        for idx, val in enumerate((-sgam, -step * c0, -step * c1, -step * c2, sgam * a0, sgam * a1, sgam * a2)):
            coef[idx] = val
        return rho0, rho1, sg0, sg1, yg0, yg1, ys1, yy0, yy1, yy11

    def load_coef():
        return [coef[idx] for idx in range(1 + 2 * HIST)]

    w2_row = jnp.broadcast_to(wout_ref[...], (hid_rows, LANES))
    w2_col = jnp.sum(jnp.where(eye, w2_row, 0.0), axis=1, keepdims=True)
    w2[...] = jnp.broadcast_to(w2_col, (hid_rows, LANES))
    w_load.wait()
    w0_w0 = jnp.zeros((SUBL, LANES), F32)
    for part in col_parts:
        w_part = w0[:, part]
        w0_w0 = w0_w0 + fold(w_part * w_part)
        store_split(split_w, part, w_part)
    peaks = []
    for idx, part in enumerate(row_parts):
        x_loads[idx].wait()
        x_part = x_v[part, :]
        prod = lax.dot_general(split_w[...], x_part, (((1,), (1,)), ((), ())), preferred_element_type=F32)
        pre_part = merge3(prod, hid_rows) * in_scale
        pre[:, part] = pre_part
        pre0[:, part] = pre_part
        peaks.append(jnp.max(jnp.abs(x_part).reshape(ROW_CHUNK // 16, 16, dim), axis=0))
    pl.semaphore_wait(barrier, n - 1)
    send_logits(z_buf.at[0], 0)
    x_scale, x_inverse = power_of_two(jnp.max(functools.reduce(jnp.maximum, peaks).astype(F32)))
    for part in row_parts:
        xs[part, :] = x_v[part, :] * jnp.full((ROW_CHUNK, dim), x_inverse, F32).astype(BF16)
    for row, row_part in enumerate(row_parts):
        for col, col_part in enumerate(row_parts[: row + 1]):
            block = lax.dot_general(
                xs[row_part, :], xs[col_part, :], (((1,), (1,)), ((), ())), preferred_element_type=F32
            ) * (in_scale * in_scale)
            for idx, term in enumerate(split3(block)):
                gram[idx, row_part, col_part] = term
            if col < row:
                for idx, term in enumerate(split3(block.T)):
                    gram[idx, col_part, row_part] = term
    for ref in (q_s, q_y, d_s, d_y, m_s, m_y, coef):
        ref[...] = jnp.zeros_like(ref)
    cv[...] = jnp.where(unit == 0, 1.0, 0.0)
    coef[0] = jnp.full((SUBL, LANES), -step, F32)
    residual(z_buf.at[0], 0)
    acc_w0 = reg * w0_w0
    for idx, part in enumerate(tiles):
        d_new = fac[:, part] * resid[idx : idx + 1, :]
        d_old[:, part] = d_new
        d_g[:, part] = d_new
        store_split(split_d, part, d_new)
        acc_w0 = acc_w0 + fold(d_new * pre0[:, part])
    m_g[sums, :] = acc_w0
    m_g[cfrow, :] = reg * cv[...] + jnp.where(unit == 1, 1.0, 0.0)
    m_g[w2rows, :] = w2_grad()
    for part in row_parts:
        q_g[:, part] = reg * pre0[:, part] + gram_times(part)
    store_loss(0)

    def head(k):
        new, old1, old2 = lax.rem(k, HIST), lax.rem(k + 2, HIST), lax.rem(k + 1, HIST)
        prev = (old1, old2, new)
        cfs = load_coef()
        move(cfs, prev)
        send_logits(z_buf.at[1], 1)
        acc_gs = move_rest(cfs, prev)
        keep_g_part(k - 1)
        residual(z_buf.at[1], 1)
        new_grad(k, (new, old1, old2), acc_gs)

    def body(k, carry):
        head(k)
        store_loss(k)
        return two_loop(carry)

    zero = jnp.zeros((SUBL, LANES), F32)
    carry = lax.fori_loop(1, NUM_ITERS - 1, body, (zero,) * 10)

    last = NUM_ITERS - 1
    head(last)
    store_loss(last)
    keep_g_part(last)
    two_loop(carry)
    slots = (last % HIST, (last + 2) % HIST, (last + 1) % HIST)
    cfs = load_coef()
    w2_new = w2[...] + combine(cfs, slots, m_g, m_s, m_y, w2rows, lanes)
    out_w2[...] = jnp.sum(jnp.where(eye, w2_new, 0.0), axis=0, keepdims=True)
    cv_new = cv[...] + combine(cfs, slots, m_g, m_s, m_y, cfrow, lanes)
    weights = [splat(cv_new[idx : idx + 1, :]) for idx in range(1 + NUM_ITERS)]
    for start in range(0, dim, LANES):
        part = pl.ds(start, LANES)

        def weighted(cf, val):
            return (val.reshape(hid_rows // SUBL, SUBL, LANES) * cf[None]).reshape(hid_rows, LANES)

        total = weighted(weights[0], w0[:, part])
        for idx in range(NUM_ITERS):
            total = total + weighted(weights[1 + idx], g_parts[idx, :, part])
        out_w[:, part] = total


def write_out(w_ref, w2_ref, loss_ref, out_w, out_w2, out_loss, sems):
    copies = [
        pltpu.make_async_copy(src, dst, sems.at[idx])
        for idx, (src, dst) in enumerate(((w_ref, out_w), (w2_ref, out_w2), (loss_ref, out_loss)))
    ]
    for copy in copies:
        copy.start()
    for copy in copies:
        copy.wait()


def solution(mesh):
    n = mesh.shape["feat"]

    def local_solve(x_loc, t_loc, win_loc, wout_loc, reg_loc, step_loc):
        num_rows, dim = x_loc.shape
        hid_rows = win_loc.shape[0]
        flat = pltpu.VMEM((hid_rows, num_rows), F32)
        past = pltpu.VMEM((HIST, hid_rows, num_rows), F32)
        meta = 2 * SUBL + hid_rows
        in_scale = 1.0 / math.sqrt(dim)
        out_scale = 1.0 / math.sqrt(hid_rows * n)
        row_tiles = num_rows // LANES
        vmem = pl.BlockSpec(memory_space=pltpu.VMEM)
        smem = pl.BlockSpec(memory_space=pltpu.SMEM)
        anym = pl.BlockSpec(memory_space=pl.ANY)
        shapes = ((hid_rows, dim), (1, hid_rows), (NUM_ITERS,))
        solved = pl.pallas_call(
            functools.partial(kernel, "feat", n, in_scale, out_scale),
            out_shape=(pltpu.VMEM(shapes[0], F32), pltpu.VMEM(shapes[1], F32), pltpu.SMEM(shapes[2], F32)),
            in_specs=[anym] * 6,
            out_specs=(vmem, vmem, smem),
            scratch_shapes=[
                pltpu.VMEM((row_tiles, LANES), F32),
                pltpu.VMEM((1, hid_rows), F32),
                pltpu.SMEM((1,), F32),
                pltpu.SMEM((1,), F32),
                pltpu.VMEM((num_rows, dim), BF16),
                pltpu.VMEM((num_rows, dim), BF16),
                pltpu.VMEM((hid_rows, dim), F32),
                pltpu.VMEM((3, num_rows, num_rows), BF16),
                pltpu.VMEM((NUM_ITERS, hid_rows, dim), F32),
                *([flat] * 5),
                past, past, flat, past, past, flat,
                pltpu.VMEM((HIST, meta, LANES), F32),
                pltpu.VMEM((HIST, meta, LANES), F32),
                pltpu.VMEM((meta, LANES), F32),
                pltpu.VMEM((hid_rows, LANES), F32),
                pltpu.VMEM((SUBL, LANES), F32),
                pltpu.VMEM((3 * hid_rows, num_rows), BF16),
                pltpu.VMEM((3 * hid_rows, dim), BF16),
                pltpu.VMEM((row_tiles, LANES), F32),
                pltpu.VMEM((row_tiles, LANES), F32),
                pltpu.VMEM((1 + 2 * HIST, SUBL, LANES), F32),
                pltpu.VMEM((row_tiles, LANES), F32),
                pltpu.VMEM((2, n, row_tiles, LANES), F32),
                pltpu.VMEM((1, LANES), F32),
                pltpu.VMEM((n, 1, LANES), F32),
                pltpu.SemaphoreType.DMA((1 + num_rows // ROW_CHUNK,)),
                pltpu.SemaphoreType.DMA((4,)),
                pltpu.SemaphoreType.DMA((3,)),
                pltpu.SemaphoreType.DMA((3,)),
            ],
            compiler_params=pltpu.CompilerParams(
                collective_id=0, has_side_effects=True, vmem_limit_bytes=61 * 1024 * 1024
            ),
        )(
            *(
                pltpu.with_memory_space_constraint(arg, pltpu.HBM)
                for arg in (x_loc, t_loc.reshape(row_tiles, LANES), win_loc, wout_loc.reshape(1, hid_rows))
            ),
            reg_loc, step_loc,
        )
        new_w, new_w2, losses = pl.pallas_call(
            write_out,
            out_shape=tuple(jax.ShapeDtypeStruct(shape, F32) for shape in shapes),
            in_specs=[vmem, vmem, smem],
            out_specs=(anym, anym, anym),
            scratch_shapes=[pltpu.SemaphoreType.DMA((3,))],
            compiler_params=pltpu.CompilerParams(vmem_limit_bytes=1024 * 1024),
        )(*solved)
        return new_w, new_w2.reshape(hid_rows), losses

    specs_in = (P("prob", None), P("prob"), P(("prob", "feat"), None), P(("prob", "feat")), P("prob"), P("prob"))
    specs_out = (P(("prob", "feat"), None), P(("prob", "feat")), P("prob"))
    return jax.shard_map(local_solve, mesh=mesh, in_specs=specs_in, out_specs=specs_out, check_vma=False)
```

time: 95.1 us -> 86 us (0.904)
  Pallas kernels: 92.9 us -> 83.8 us
    pallas_call x1, Pallas kernels: 91.7 us -> 82.7 us  [local_solve(): pl.pallas_call(functools.partial(kernel, 'feat', n, in_scale, out_scale),...]
where the time goes in v3:
time: 86 us; the launch traced here: 85.9 us
  Pallas kernels  83.8 us (97%)
  between operations  2.09 us (2%)
    pallas_call x1, Pallas kernels, local_solve(): pl.pallas_call(functools.partial(kernel, 'feat', n, in_scale, out_scale),...  82.7 us

profile of v3, /device:TPU:21, one launch (start us, length us, event | category | flops | bytes accessed | tf_op | source)
XLA Modules:
  0.0 85.9 jit_solution(1536607585571862781)
XLA Ops:
  1.9 82.7 %shard_map.85 = (f32[128,3072]{1,0:T(8,128)S(1)}, f32[1,128]{1,0:T(1,128)S(1)}, f32[6]{0:T(128)S(4)}) custom-call(bf16[1024,3072]{1,0:T(8,128)(2,1)} %x_hbm.1, f32[8,128]{1,0:T(8,128)} %bitcast.3, f32[128,3072]{1,0:T(8,128)} %win_hbm.1, f32[1,128]{1,0:T(1,128)} %bitcast.4, f32[1]{0:T(128)S(6)} %copy.9.reg_hbm, f32[1]{0:T(128)S(6)} %copy.10.step_hbm), custom_call_target="tpu_custom_call" | custom-call | tf_op jit(solution)/shard_map/pallas_call | solution.py:397
  84.6 1.2 %shard_map.86 = (f32[128,3072]{1,0:T(8,128)}, f32[1,128]{1,0:T(1,128)}, f32[6]{0:T(128)}) custom-call(f32[128,3072]{1,0:T(8,128)S(1)} %get-tuple-element.9.w_ref, f32[1,128]{1,0:T(1,128)S(1)} %get-tuple-element.10.w2_ref, f32[6]{0:T(128)S(4)} %get-tuple-element.11.loss_ref), custom_call_target="tpu_custom_call" | custom-call | tf_op jit(solution)/shard_map/pallas_call | solution.py:443

commit v4 on v3

--- a/solution.py
+++ b/solution.py
@@ -58,9 +58,9 @@
 def kernel(
     axis, n, in_scale, out_scale,
     x_hbm, t_hbm, win_hbm, wout_hbm, reg_hbm, step_hbm,
-    out_w, out_w2, out_loss,
+    w0, g_parts, weights, out_w2, out_loss,
     t_ref, wout_ref, reg_ref, step_ref,
-    x_v, xs, w0, gram, g_parts, pre, pre0, hid, fac, d_old,
+    x_v, xs, gram, pre, pre0, hid, fac, d_old,
     q_s, q_y, q_g, d_s, d_y, d_g, m_s, m_y, m_g, w2, cv,
     split_d, split_w, resid, logits_v, coef,
     z_src, z_buf, dot_src, dot_buf,
@@ -73,7 +73,7 @@
     offsets = sorted(range(1, n), key=lambda off: -min(off, n - off))
     peers = [lax.rem(me + off, n) for off in offsets]
 
-    w_load = pltpu.make_async_copy(win_hbm, w0, load_sem.at[0])
+    w_load = pltpu.make_async_copy(win_hbm, w0.at[:, pl.ds(0, dim)], load_sem.at[0])
     w_load.start()
     x_loads = []
     row_parts = [pl.ds(start, ROW_CHUNK) for start in range(0, num_rows, ROW_CHUNK)]
@@ -278,7 +278,8 @@
     w2[...] = jnp.broadcast_to(w2_col, (hid_rows, LANES))
     w_load.wait()
     w0_w0 = jnp.zeros((SUBL, LANES), F32)
-    for part in col_parts:
+    for start in range(0, dim, LANES):
+        part = pl.ds(start, LANES)
         w_part = w0[:, part]
         w0_w0 = w0_w0 + fold(w_part * w_part)
         store_split(split_w, part, w_part)
@@ -354,26 +355,33 @@
     w2_new = w2[...] + combine(cfs, slots, m_g, m_s, m_y, w2rows, lanes)
     out_w2[...] = jnp.sum(jnp.where(eye, w2_new, 0.0), axis=0, keepdims=True)
     cv_new = cv[...] + combine(cfs, slots, m_g, m_s, m_y, cfrow, lanes)
-    weights = [splat(cv_new[idx : idx + 1, :]) for idx in range(1 + NUM_ITERS)]
-    for start in range(0, dim, LANES):
-        part = pl.ds(start, LANES)
-
-        def weighted(cf, val):
-            return (val.reshape(hid_rows // SUBL, SUBL, LANES) * cf[None]).reshape(hid_rows, LANES)
-
-        total = weighted(weights[0], w0[:, part])
-        for idx in range(NUM_ITERS):
-            total = total + weighted(weights[1 + idx], g_parts[idx, :, part])
-        out_w[:, part] = total
-
-
-def write_out(w_ref, w2_ref, loss_ref, out_w, out_w2, out_loss, sems):
+    for idx in range(1 + NUM_ITERS):
+        weights[idx] = splat(cv_new[idx : idx + 1, :])
+
+
+def write_out(w0, g_parts, weights, w2_ref, loss_ref, out_w, out_w2, out_loss, w_v, sems, w_sems):
+    rows, dim = out_w.shape
     copies = [
-        pltpu.make_async_copy(src, dst, sems.at[idx])
-        for idx, (src, dst) in enumerate(((w_ref, out_w), (w2_ref, out_w2), (loss_ref, out_loss)))
+        pltpu.make_async_copy(src, dst, sems.at[idx]) for idx, (src, dst) in enumerate(((w2_ref, out_w2), (loss_ref, out_loss)))
     ]
     for copy in copies:
         copy.start()
+    factors = [weights[idx][None] for idx in range(1 + NUM_ITERS)]
+
+    def weighted(factor, val):
+        return (val.reshape(rows // SUBL, SUBL, LANES) * factor).reshape(rows, LANES)
+
+    for idx, start in enumerate(range(0, dim, COL_CHUNK)):
+        for tile in range(start, start + COL_CHUNK, LANES):
+            part = pl.ds(tile, LANES)
+            total = weighted(factors[0], w0[:, part])
+            for term in range(NUM_ITERS):
+                total = total + weighted(factors[1 + term], g_parts[term, :, part])
+            w_v[:, part] = total
+        part = pl.ds(start, COL_CHUNK)
+        copy = pltpu.make_async_copy(w_v.at[:, part], out_w.at[:, part], w_sems.at[idx])
+        copy.start()
+        copies.append(copy)
     for copy in copies:
         copy.wait()
 
@@ -384,8 +392,8 @@
     def local_solve(x_loc, t_loc, win_loc, wout_loc, reg_loc, step_loc):
         num_rows, dim = x_loc.shape
         hid_rows = win_loc.shape[0]
-        flat = pltpu.VMEM((hid_rows, num_rows), F32)
-        past = pltpu.VMEM((HIST, hid_rows, num_rows), F32)
+        flat = pltpu.VMEM((hid_rows, num_rows + LANES), F32)
+        past = pltpu.VMEM((HIST, hid_rows, num_rows + LANES), F32)
         meta = 2 * SUBL + hid_rows
         in_scale = 1.0 / math.sqrt(dim)
         out_scale = 1.0 / math.sqrt(hid_rows * n)
@@ -393,12 +401,17 @@
         vmem = pl.BlockSpec(memory_space=pltpu.VMEM)
         smem = pl.BlockSpec(memory_space=pltpu.SMEM)
         anym = pl.BlockSpec(memory_space=pl.ANY)
-        shapes = ((hid_rows, dim), (1, hid_rows), (NUM_ITERS,))
         solved = pl.pallas_call(
             functools.partial(kernel, "feat", n, in_scale, out_scale),
-            out_shape=(pltpu.VMEM(shapes[0], F32), pltpu.VMEM(shapes[1], F32), pltpu.SMEM(shapes[2], F32)),
+            out_shape=(
+                pltpu.VMEM((hid_rows, dim + LANES), F32),
+                pltpu.VMEM((NUM_ITERS, hid_rows, dim + LANES), F32),
+                pltpu.VMEM((1 + NUM_ITERS, SUBL, LANES), F32),
+                pltpu.VMEM((1, hid_rows), F32),
+                pltpu.SMEM((NUM_ITERS,), F32),
+            ),
             in_specs=[anym] * 6,
-            out_specs=(vmem, vmem, smem),
+            out_specs=(vmem, vmem, vmem, vmem, smem),
             scratch_shapes=[
                 pltpu.VMEM((row_tiles, LANES), F32),
                 pltpu.VMEM((1, hid_rows), F32),
@@ -406,9 +419,7 @@
                 pltpu.SMEM((1,), F32),
                 pltpu.VMEM((num_rows, dim), BF16),
                 pltpu.VMEM((num_rows, dim), BF16),
-                pltpu.VMEM((hid_rows, dim), F32),
                 pltpu.VMEM((3, num_rows, num_rows), BF16),
-                pltpu.VMEM((NUM_ITERS, hid_rows, dim), F32),
                 *([flat] * 5),
                 past, past, flat, past, past, flat,
                 pltpu.VMEM((HIST, meta, LANES), F32),
@@ -431,7 +442,7 @@
                 pltpu.SemaphoreType.DMA((3,)),
             ],
             compiler_params=pltpu.CompilerParams(
-                collective_id=0, has_side_effects=True, vmem_limit_bytes=61 * 1024 * 1024
+                collective_id=0, has_side_effects=True, vmem_limit_bytes=46 * 1024 * 1024
             ),
         )(
             *(
@@ -442,11 +453,15 @@
         )
         new_w, new_w2, losses = pl.pallas_call(
             write_out,
-            out_shape=tuple(jax.ShapeDtypeStruct(shape, F32) for shape in shapes),
-            in_specs=[vmem, vmem, smem],
+            out_shape=tuple(jax.ShapeDtypeStruct(shape, F32) for shape in ((hid_rows, dim), (1, hid_rows), (NUM_ITERS,))),
+            in_specs=[vmem, vmem, vmem, vmem, smem],
             out_specs=(anym, anym, anym),
-            scratch_shapes=[pltpu.SemaphoreType.DMA((3,))],
-            compiler_params=pltpu.CompilerParams(vmem_limit_bytes=1024 * 1024),
+            scratch_shapes=[
+                pltpu.VMEM((hid_rows, dim + LANES), F32),
+                pltpu.SemaphoreType.DMA((2,)),
+                pltpu.SemaphoreType.DMA((dim // COL_CHUNK,)),
+            ],
+            compiler_params=pltpu.CompilerParams(vmem_limit_bytes=4 * 1024 * 1024),
         )(*solved)
         return new_w, new_w2.reshape(hid_rows), losses
 

time: 86 us -> 84 us (0.977)
  Pallas kernels: 83.8 us -> 81.7 us
    pallas_call x1, Pallas kernels: 82.7 us -> 80.3 us  [local_solve(): pl.pallas_call(functools.partial(kernel, 'feat', n, in_scale, out_scale),...]
where the time goes in v4:
time: 84 us; the launch traced here: 83.8 us
  Pallas kernels  81.7 us (97%)
  between operations  2.09 us (2%)
    pallas_call x1, Pallas kernels, local_solve(): pl.pallas_call(functools.partial(kernel, 'feat', n, in_scale, out_scale),...  80.3 us

profile of v4, /device:TPU:21, one launch (start us, length us, event | category | flops | bytes accessed | tf_op | source)
XLA Modules:
  0.0 83.8 jit_solution(3731338749372532070)
XLA Ops:
  1.9 80.3 %shard_map.85 = (f32[128,3200]{1,0:T(8,128)S(1)}, f32[6,128,3200]{2,1,0:T(8,128)S(1)}, f32[7,8,128]{2,1,0:T(8,128)S(1)}, f32[1,128]{1,0:T(1,128)S(1)}, f32[6]{0:T(128)S(4)}) custom-call(bf16[1024,3072]{1,0:T(8,128)(2,1)} %x_hbm.1, f32[8,128]{1,0:T(8,128)} %bitcast.3, f32[128,3072]{1,0:T(8,128)} %win_hbm.1, f32[1,128]{1,0:T(1,128)} %bitcast.4, ...), custom_call_target="tpu_custom_call" | custom-call | tf_op jit(solution)/shard_map/pallas_call | solution.py:404
  82.2 1.4 %shard_map.86 = (f32[128,3072]{1,0:T(8,128)}, f32[1,128]{1,0:T(1,128)}, f32[6]{0:T(128)}) custom-call(f32[128,3200]{1,0:T(8,128)S(1)} %get-tuple-element.11.w0, f32[6,128,3200]{2,1,0:T(8,128)S(1)} %get-tuple-element.12.g_parts, f32[7,8,128]{2,1,0:T(8,128)S(1)} %get-tuple-element.13.weights, f32[1,128]{1,0:T(1,128)S(1)} %get-tuple-element.14.w2_ref, ...), custom_call_target="tpu_custom_call" | custom-call | tf_op jit(solution)/shard_map/pallas_call | solution.py:454

commit v5 on v4

--- a/solution.py
+++ b/solution.py
@@ -62,14 +62,18 @@
     t_ref, wout_ref, reg_ref, step_ref,
     x_v, xs, gram, pre, pre0, hid, fac, d_old,
     q_s, q_y, q_g, d_s, d_y, d_g, m_s, m_y, m_g, w2, cv,
-    split_d, split_w, resid, logits_v, coef,
-    z_src, z_buf, dot_src, dot_buf,
+    split_d, split_w, resid, k_part, coef,
+    z_src, z_buf, half_src, half_buf, dot_src, dot_buf,
     load_sem, small_sem, send_sem, recv_sem,
 ):
     num_rows, dim = x_v.shape
     hid_rows = w0.shape[0]
     row_tiles = num_rows // LANES
+    half_tiles = row_tiles // 2
+    half_rows = num_rows // 2
     me = lax.axis_index(axis)
+    own = lax.rem(me, 2)
+    partner = me + 1 - 2 * own
     offsets = sorted(range(1, n), key=lambda off: -min(off, n - off))
     peers = [lax.rem(me + off, n) for off in offsets]
 
@@ -109,6 +113,13 @@
                 device_id={axis: peer}, device_id_type=MESH,
             ).start()
 
+    def send_halves(buf, sem):
+        for peer in peers:
+            pltpu.make_async_remote_copy(
+                src_ref=z_src.at[lax.rem(peer, 2)], dst_ref=buf.at[me], send_sem=send_sem.at[sem],
+                recv_sem=recv_sem.at[sem], device_id={axis: peer}, device_id_type=MESH,
+            ).start()
+
     def wait_all(dst, sem):
         others = dst.at[pl.ds(0, n - 1)]
         pltpu.make_async_copy(others, others, recv_sem.at[sem]).wait()
@@ -127,42 +138,69 @@
             act = jnp.tanh(pre[:, part])
             hid[:, part] = act
             rows.append(jnp.sum(fold(act * w2[...]), axis=0, keepdims=True))
-        z_mine = jnp.concatenate(rows, axis=0)
-        z_src[...] = z_mine
-        buf[me] = z_mine
-        send_all(z_src, buf, sem)
+        z_src[0] = jnp.concatenate(rows[:half_tiles], axis=0)
+        z_src[1] = jnp.concatenate(rows[half_tiles:], axis=0)
+        buf[me] = z_src[own]
+        send_halves(buf, sem)
         w2s = w2[...] * out_scale
         for part in tiles:
             act = hid[:, part]
             fac[:, part] = w2s * (1.0 - act * act)
 
-    def residual(buf, sem):
+    def gram_times(buf, sem, on_tile, after_tiles, finish):
         wait_all(buf, sem)
         logits = jnp.sum(buf[...], axis=0) * out_scale
-        logits_v[...] = logits
-        resid[...] = (jax.nn.sigmoid(logits) - t_ref[...]) * (1.0 / num_rows)
+        half_src[...] = logits
+        half_buf[own] = logits
+        swap = pltpu.make_async_remote_copy(
+            src_ref=half_src, dst_ref=half_buf.at[own], send_sem=send_sem.at[3], recv_sem=recv_sem.at[3],
+            device_id={axis: partner}, device_id_type=MESH,
+        )
+        swap.start()
+        for slot, half in enumerate((own, 1 - own)):
+            if slot:
+                swap.wait()
+                logits = half_buf[half]
+            res = (jax.nn.sigmoid(logits) - t_ref[half]) * (1.0 / num_rows)
+            resid[half] = res
+            parts = []
+            for idx in range(half_tiles):
+                part = pl.ds(pl.multiple_of(half * half_rows + idx * LANES, LANES), LANES)
+                parts.append(part)
+                diff = on_tile(part, fac[:, part] * res[idx : idx + 1, :])
+                for row, term in enumerate(split3(diff)):
+                    split_d[slot, row * hid_rows : (row + 1) * hid_rows, idx * LANES : (idx + 1) * LANES] = term
+            after_tiles(parts)
+            rows = pl.ds(pl.multiple_of(half * half_rows, half_rows), half_rows)
+            for part in row_parts:
+                high = jnp.dot(split_d[slot], gram[0, rows, part], preferred_element_type=F32)
+                mid = jnp.dot(split_d[slot, : 2 * hid_rows], gram[1, rows, part], preferred_element_type=F32)
+                low = jnp.dot(split_d[slot, :hid_rows], gram[2, rows, part], preferred_element_type=F32)
+                small = (high[2 * hid_rows :] + mid[hid_rows:]) + low
+                total = ((high[hid_rows : 2 * hid_rows] + mid[:hid_rows]) + small) + high[:hid_rows]
+                if slot:
+                    finish(part, ((total + k_part[:, part]) * x_scale) * x_scale)
+                else:
+                    k_part[:, part] = total
 
     def w2_grad():
-        total = hid[:, tiles[0]] * resid[0:1, :]
+        total = hid[:, tiles[0]] * resid[0, 0:1, :]
         for idx in range(1, row_tiles):
-            total = total + hid[:, tiles[idx]] * resid[idx : idx + 1, :]
+            half, row = divmod(idx, half_tiles)
+            total = total + hid[:, tiles[idx]] * resid[half, row : row + 1, :]
         g_out = jnp.sum(total, axis=1, keepdims=True) * out_scale
         return jnp.broadcast_to(g_out, (hid_rows, LANES)) + reg * w2[...]
 
-    def gram_times(part):
-        high = jnp.dot(split_d[...], gram[0, :, part], preferred_element_type=F32)
-        mid = jnp.dot(split_d[: 2 * hid_rows], gram[1, :, part], preferred_element_type=F32)
-        low = jnp.dot(split_d[:hid_rows], gram[2, :, part], preferred_element_type=F32)
-        small = (high[2 * hid_rows :] + mid[hid_rows:]) + low
-        return (((high[hid_rows : 2 * hid_rows] + mid[:hid_rows]) + small + high[:hid_rows]) * x_scale) * x_scale
-
     def keep_g_part(idx):
         for part in col_parts:
-            prod = jnp.dot(split_d[...], xs[:, part], preferred_element_type=F32)
-            g_parts[idx, :, part] = merge3(prod, hid_rows) * in_scale * x_scale
+            prods = []
+            for slot, half in enumerate((own, 1 - own)):
+                rows = pl.ds(pl.multiple_of(half * half_rows, half_rows), half_rows)
+                prods.append(jnp.dot(split_d[slot], xs[rows, part], preferred_element_type=F32))
+            g_parts[idx, :, part] = merge3(prods[0] + prods[1], hid_rows) * in_scale * x_scale
 
     def store_loss(idx):
-        logits = logits_v[...]
+        logits = half_buf[...]
         soft = jnp.maximum(logits, 0.0) + jnp.log1p(jnp.exp(-jnp.abs(logits)))
         out_loss[idx] = jnp.sum(soft - t_ref[...] * logits) * (1.0 / num_rows)
 
@@ -203,37 +241,43 @@
 
     def new_grad(k, slots, acc_gs):
         new, old1, old2 = slots
-        w2_part = w2_grad() - m_g[w2rows, :]
-        acc_w0 = jnp.zeros((SUBL, LANES), F32)
-        for idx, part in enumerate(tiles):
-            d_new = fac[:, part] * resid[idx : idx + 1, :]
+        others = [(q_s, m_s, new), (q_s, m_s, old1), (q_s, m_s, old2), (q_y, m_y, old1), (q_y, m_y, old2)]
+        zero = jnp.zeros((SUBL, LANES), F32)
+        accs = [zero] * len(others)
+        rest = {"w0": zero, "gp": zero, "yy": zero}
+
+        def on_tile(part, d_new):
             diff = d_new - d_old[:, part]
             d_old[:, part] = d_new
-            store_split(split_d, part, diff)
             d_y[new, :, part] = reg * d_s[new, :, part] + diff
-            acc_w0 = acc_w0 + fold(diff * pre0[:, part])
-        w0_y = reg * m_s[new, sums, :] + acc_w0
+            rest["w0"] = rest["w0"] + fold(diff * pre0[:, part])
+            return diff
+
+        def after_tiles(parts):
+            for part in parts:
+                d_part = d_y[new, :, part]
+                for idx, (q, _, slot) in enumerate(others):
+                    accs[idx] = accs[idx] + fold(d_part * q[slot, :, part])
+                rest["gp"] = rest["gp"] + fold(d_part * q_g[:, part])
+
+        def finish(part, val):
+            q_new = reg * q_s[new, :, part] + val
+            q_y[new, :, part] = q_new
+            q_g[:, part] = q_g[:, part] + q_new
+            rest["yy"] = rest["yy"] + fold(d_y[new, :, part] * q_new)
+
+        gram_times(z_buf.at[1], 1, on_tile, after_tiles, finish)
+        w2_part = w2_grad() - m_g[w2rows, :]
+        w0_y = reg * m_s[new, sums, :] + rest["w0"]
         cf_y = reg * m_s[new, cfrow, :] + jnp.where(unit == k + 1, 1.0, 0.0)
         c_y = splat(cf_y[0:1, :])
         m_y[new, sums, :] = w0_y
         m_y[new, cfrow, :] = cf_y
         m_y[new, w2rows, :] = w2_part
-        others = [(q_s, m_s, new), (q_s, m_s, old1), (q_s, m_s, old2), (q_y, m_y, old1), (q_y, m_y, old2)]
-        accs = [
-            c_y * m[slot, sums, :] + fold(w2_part * m[slot, w2rows, :]) * (1.0 / LANES) for _, m, slot in others
-        ]
-        acc_gp = c_y * m_g[sums, :] + fold(w2_part * m_g[w2rows, :]) * (1.0 / LANES)
-        acc_yy = c_y * w0_y + fold(w2_part * w2_part) * (1.0 / LANES)
-        for part in row_parts:
-            d_part = d_y[new, :, part]
-            for idx, (q, _, slot) in enumerate(others):
-                accs[idx] = accs[idx] + fold(d_part * q[slot, :, part])
-            q_old = q_g[:, part]
-            acc_gp = acc_gp + fold(d_part * q_old)
-            q_new = reg * q_s[new, :, part] + gram_times(part)
-            q_y[new, :, part] = q_new
-            q_g[:, part] = q_old + q_new
-            acc_yy = acc_yy + fold(d_part * q_new)
+        for idx, (_, m, slot) in enumerate(others):
+            accs[idx] = accs[idx] + c_y * m[slot, sums, :] + fold(w2_part * m[slot, w2rows, :]) * (1.0 / LANES)
+        acc_gp = rest["gp"] + c_y * m_g[sums, :] + fold(w2_part * m_g[w2rows, :]) * (1.0 / LANES)
+        acc_yy = rest["yy"] + c_y * w0_y + fold(w2_part * w2_part) * (1.0 / LANES)
         order = accs[:3] + [acc_yy] + accs[3:] + [acc_gp, acc_gs]
         rows = [jnp.sum(acc, axis=0, keepdims=True) for acc in order]
         totals = jnp.sum(jnp.concatenate(rows, axis=0), axis=1, keepdims=True)
@@ -311,19 +355,21 @@
         ref[...] = jnp.zeros_like(ref)
     cv[...] = jnp.where(unit == 0, 1.0, 0.0)
     coef[0] = jnp.full((SUBL, LANES), -step, F32)
-    residual(z_buf.at[0], 0)
-    acc_w0 = reg * w0_w0
-    for idx, part in enumerate(tiles):
-        d_new = fac[:, part] * resid[idx : idx + 1, :]
+    first = {"w0": reg * w0_w0}
+
+    def first_tile(part, d_new):
         d_old[:, part] = d_new
         d_g[:, part] = d_new
-        store_split(split_d, part, d_new)
-        acc_w0 = acc_w0 + fold(d_new * pre0[:, part])
-    m_g[sums, :] = acc_w0
+        first["w0"] = first["w0"] + fold(d_new * pre0[:, part])
+        return d_new
+
+    def first_q(part, val):
+        q_g[:, part] = reg * pre0[:, part] + val
+
+    gram_times(z_buf.at[0], 0, first_tile, lambda parts: None, first_q)
+    m_g[sums, :] = first["w0"]
     m_g[cfrow, :] = reg * cv[...] + jnp.where(unit == 1, 1.0, 0.0)
     m_g[w2rows, :] = w2_grad()
-    for part in row_parts:
-        q_g[:, part] = reg * pre0[:, part] + gram_times(part)
     store_loss(0)
 
     def head(k):
@@ -334,7 +380,6 @@
         send_logits(z_buf.at[1], 1)
         acc_gs = move_rest(cfs, prev)
         keep_g_part(k - 1)
-        residual(z_buf.at[1], 1)
         new_grad(k, (new, old1, old2), acc_gs)
 
     def body(k, carry):
@@ -394,10 +439,11 @@
         hid_rows = win_loc.shape[0]
         flat = pltpu.VMEM((hid_rows, num_rows + LANES), F32)
         past = pltpu.VMEM((HIST, hid_rows, num_rows + LANES), F32)
+        row_tiles = num_rows // LANES
+        halves = pltpu.VMEM((2, row_tiles // 2, LANES), F32)
         meta = 2 * SUBL + hid_rows
         in_scale = 1.0 / math.sqrt(dim)
         out_scale = 1.0 / math.sqrt(hid_rows * n)
-        row_tiles = num_rows // LANES
         vmem = pl.BlockSpec(memory_space=pltpu.VMEM)
         smem = pl.BlockSpec(memory_space=pltpu.SMEM)
         anym = pl.BlockSpec(memory_space=pl.ANY)
@@ -413,7 +459,7 @@
             in_specs=[anym] * 6,
             out_specs=(vmem, vmem, vmem, vmem, smem),
             scratch_shapes=[
-                pltpu.VMEM((row_tiles, LANES), F32),
+                halves,
                 pltpu.VMEM((1, hid_rows), F32),
                 pltpu.SMEM((1,), F32),
                 pltpu.SMEM((1,), F32),
@@ -427,19 +473,21 @@
                 pltpu.VMEM((meta, LANES), F32),
                 pltpu.VMEM((hid_rows, LANES), F32),
                 pltpu.VMEM((SUBL, LANES), F32),
-                pltpu.VMEM((3 * hid_rows, num_rows), BF16),
+                pltpu.VMEM((2, 3 * hid_rows, num_rows // 2), BF16),
                 pltpu.VMEM((3 * hid_rows, dim), BF16),
-                pltpu.VMEM((row_tiles, LANES), F32),
-                pltpu.VMEM((row_tiles, LANES), F32),
+                halves,
+                flat,
                 pltpu.VMEM((1 + 2 * HIST, SUBL, LANES), F32),
-                pltpu.VMEM((row_tiles, LANES), F32),
-                pltpu.VMEM((2, n, row_tiles, LANES), F32),
+                halves,
+                pltpu.VMEM((2, n, row_tiles // 2, LANES), F32),
+                pltpu.VMEM((row_tiles // 2, LANES), F32),
+                halves,
                 pltpu.VMEM((1, LANES), F32),
                 pltpu.VMEM((n, 1, LANES), F32),
                 pltpu.SemaphoreType.DMA((1 + num_rows // ROW_CHUNK,)),
                 pltpu.SemaphoreType.DMA((4,)),
-                pltpu.SemaphoreType.DMA((3,)),
-                pltpu.SemaphoreType.DMA((3,)),
+                pltpu.SemaphoreType.DMA((4,)),
+                pltpu.SemaphoreType.DMA((4,)),
             ],
             compiler_params=pltpu.CompilerParams(
                 collective_id=0, has_side_effects=True, vmem_limit_bytes=46 * 1024 * 1024
@@ -447,7 +495,7 @@
         )(
             *(
                 pltpu.with_memory_space_constraint(arg, pltpu.HBM)
-                for arg in (x_loc, t_loc.reshape(row_tiles, LANES), win_loc, wout_loc.reshape(1, hid_rows))
+                for arg in (x_loc, t_loc.reshape(2, row_tiles // 2, LANES), win_loc, wout_loc.reshape(1, hid_rows))
             ),
             reg_loc, step_loc,
         )

time: 84 us -> 85.8 us (1.021)
  Pallas kernels: 81.7 us -> 83.6 us
    pallas_call x1, Pallas kernels: 80.3 us -> 82.2 us  [local_solve(): pl.pallas_call(functools.partial(kernel, 'feat', n, in_scale, out_scale),...]
where the time goes in v5:
time: 85.8 us; the launch traced here: 85.7 us
  Pallas kernels  83.6 us (97%)
  between operations  2.09 us (2%)
    pallas_call x1, Pallas kernels, local_solve(): pl.pallas_call(functools.partial(kernel, 'feat', n, in_scale, out_scale),...  82.2 us

profile of v5, /device:TPU:21, one launch (start us, length us, event | category | flops | bytes accessed | tf_op | source)
XLA Modules:
  0.0 85.7 jit_solution(12578239294881036718)
XLA Ops:
  1.9 82.2 %shard_map.85 = (f32[128,3200]{1,0:T(8,128)S(1)}, f32[6,128,3200]{2,1,0:T(8,128)S(1)}, f32[7,8,128]{2,1,0:T(8,128)S(1)}, f32[1,128]{1,0:T(1,128)S(1)}, f32[6]{0:T(128)S(4)}) custom-call(bf16[1024,3072]{1,0:T(8,128)(2,1)} %x_hbm.1, f32[2,4,128]{2,1,0:T(4,128)} %bitcast.3, f32[128,3072]{1,0:T(8,128)} %win_hbm.1, f32[1,128]{1,0:T(1,128)} %bitcast.4, ...), custom_call_target="tpu_custom_call" | custom-call | tf_op jit(solution)/shard_map/pallas_call | solution.py:450
  84.1 1.4 %shard_map.86 = (f32[128,3072]{1,0:T(8,128)}, f32[1,128]{1,0:T(1,128)}, f32[6]{0:T(128)}) custom-call(f32[128,3200]{1,0:T(8,128)S(1)} %get-tuple-element.11.w0, f32[6,128,3200]{2,1,0:T(8,128)S(1)} %get-tuple-element.12.g_parts, f32[7,8,128]{2,1,0:T(8,128)S(1)} %get-tuple-element.13.weights, f32[1,128]{1,0:T(1,128)S(1)} %get-tuple-element.14.w2_ref, ...), custom_call_target="tpu_custom_call" | custom-call | tf_op jit(solution)/shard_map/pallas_call | solution.py:502

commit v6 on v4

--- a/solution.py
+++ b/solution.py
@@ -102,8 +102,10 @@
     sums, cfrow, w2rows = pl.ds(0, SUBL), pl.ds(SUBL, SUBL), pl.ds(2 * SUBL, hid_rows)
     top = pl.ds(SUBL, 1)
 
-    def send_all(src, dst, sem):
-        for peer in peers:
+    far = sum(1 for off in offsets if min(off, n - off) > n // 4)
+
+    def send_all(src, dst, sem, targets=peers):
+        for peer in targets:
             pltpu.make_async_remote_copy(
                 src_ref=src, dst_ref=dst.at[me], send_sem=send_sem.at[sem], recv_sem=recv_sem.at[sem],
                 device_id={axis: peer}, device_id_type=MESH,
@@ -130,7 +132,7 @@
         z_mine = jnp.concatenate(rows, axis=0)
         z_src[...] = z_mine
         buf[me] = z_mine
-        send_all(z_src, buf, sem)
+        send_all(z_src, buf, sem, peers[:far])
         w2s = w2[...] * out_scale
         for part in tiles:
             act = hid[:, part]
@@ -156,8 +158,11 @@
         small = (high[2 * hid_rows :] + mid[hid_rows:]) + low
         return (((high[hid_rows : 2 * hid_rows] + mid[:hid_rows]) + small + high[:hid_rows]) * x_scale) * x_scale
 
-    def keep_g_part(idx):
-        for part in col_parts:
+    def send_near(buf, sem):
+        send_all(z_src, buf, sem, peers[far:])
+
+    def keep_g_part(idx, parts=col_parts):
+        for part in parts:
             prod = jnp.dot(split_d[...], xs[:, part], preferred_element_type=F32)
             g_parts[idx, :, part] = merge3(prod, hid_rows) * in_scale * x_scale
 
@@ -297,6 +302,7 @@
     x_scale, x_inverse = power_of_two(jnp.max(functools.reduce(jnp.maximum, peaks).astype(F32)))
     for part in row_parts:
         xs[part, :] = x_v[part, :] * jnp.full((ROW_CHUNK, dim), x_inverse, F32).astype(BF16)
+    send_near(z_buf.at[0], 0)
     for row, row_part in enumerate(row_parts):
         for col, col_part in enumerate(row_parts[: row + 1]):
             block = lax.dot_general(
@@ -333,7 +339,9 @@
         move(cfs, prev)
         send_logits(z_buf.at[1], 1)
         acc_gs = move_rest(cfs, prev)
-        keep_g_part(k - 1)
+        keep_g_part(k - 1, col_parts[:1])
+        send_near(z_buf.at[1], 1)
+        keep_g_part(k - 1, col_parts[1:])
         residual(z_buf.at[1], 1)
         new_grad(k, (new, old1, old2), acc_gs)
 

time: 84 us -> 84.3 us (level)
  no operation moved by 1% of the time
where the time goes in v6:
time: 84.3 us; the launch traced here: 84.2 us
  Pallas kernels  82.1 us (97%)
  between operations  2.09 us (2%)
    pallas_call x1, Pallas kernels, local_solve(): pl.pallas_call(functools.partial(kernel, 'feat', n, in_scale, out_scale),...  80.7 us

profile of v6, /device:TPU:21, one launch (start us, length us, event | category | flops | bytes accessed | tf_op | source)
XLA Modules:
  0.0 84.2 jit_solution(1922474444394836824)
XLA Ops:
  1.9 80.7 %shard_map.85 = (f32[128,3200]{1,0:T(8,128)S(1)}, f32[6,128,3200]{2,1,0:T(8,128)S(1)}, f32[7,8,128]{2,1,0:T(8,128)S(1)}, f32[1,128]{1,0:T(1,128)S(1)}, f32[6]{0:T(128)S(4)}) custom-call(bf16[1024,3072]{1,0:T(8,128)(2,1)} %x_hbm.1, f32[8,128]{1,0:T(8,128)} %bitcast.3, f32[128,3072]{1,0:T(8,128)} %win_hbm.1, f32[1,128]{1,0:T(1,128)} %bitcast.4, ...), custom_call_target="tpu_custom_call" | custom-call | tf_op jit(solution)/shard_map/pallas_call | solution.py:412
  82.6 1.4 %shard_map.86 = (f32[128,3072]{1,0:T(8,128)}, f32[1,128]{1,0:T(1,128)}, f32[6]{0:T(128)}) custom-call(f32[128,3200]{1,0:T(8,128)S(1)} %get-tuple-element.11.w0, f32[6,128,3200]{2,1,0:T(8,128)S(1)} %get-tuple-element.12.g_parts, f32[7,8,128]{2,1,0:T(8,128)S(1)} %get-tuple-element.13.weights, f32[1,128]{1,0:T(1,128)S(1)} %get-tuple-element.14.w2_ref, ...), custom_call_target="tpu_custom_call" | custom-call | tf_op jit(solution)/shard_map/pallas_call | solution.py:462

commit v7 on v5

--- a/solution.py
+++ b/solution.py
@@ -63,7 +63,7 @@
     x_v, xs, gram, pre, pre0, hid, fac, d_old,
     q_s, q_y, q_g, d_s, d_y, d_g, m_s, m_y, m_g, w2, cv,
     split_d, split_w, resid, k_part, coef,
-    z_src, z_buf, half_src, half_buf, dot_src, dot_buf,
+    z_src, z_buf, logits_v, dot_src, dot_buf,
     load_sem, small_sem, send_sem, recv_sem,
 ):
     num_rows, dim = x_v.shape
@@ -72,8 +72,6 @@
     half_tiles = row_tiles // 2
     half_rows = num_rows // 2
     me = lax.axis_index(axis)
-    own = lax.rem(me, 2)
-    partner = me + 1 - 2 * own
     offsets = sorted(range(1, n), key=lambda off: -min(off, n - off))
     peers = [lax.rem(me + off, n) for off in offsets]
 
@@ -106,20 +104,15 @@
     sums, cfrow, w2rows = pl.ds(0, SUBL), pl.ds(SUBL, SUBL), pl.ds(2 * SUBL, hid_rows)
     top = pl.ds(SUBL, 1)
 
-    def send_all(src, dst, sem):
-        for peer in peers:
+    far = sum(1 for off in offsets if min(off, n - off) > n // 4)
+
+    def send_all(src, dst, sem, targets=peers):
+        for peer in targets:
             pltpu.make_async_remote_copy(
                 src_ref=src, dst_ref=dst.at[me], send_sem=send_sem.at[sem], recv_sem=recv_sem.at[sem],
                 device_id={axis: peer}, device_id_type=MESH,
             ).start()
 
-    def send_halves(buf, sem):
-        for peer in peers:
-            pltpu.make_async_remote_copy(
-                src_ref=z_src.at[lax.rem(peer, 2)], dst_ref=buf.at[me], send_sem=send_sem.at[sem],
-                recv_sem=recv_sem.at[sem], device_id={axis: peer}, device_id_type=MESH,
-            ).start()
-
     def wait_all(dst, sem):
         others = dst.at[pl.ds(0, n - 1)]
         pltpu.make_async_copy(others, others, recv_sem.at[sem]).wait()
@@ -132,53 +125,45 @@
         for idx, term in enumerate(split3(val)):
             ref[idx * hid_rows : (idx + 1) * hid_rows, part] = term
 
-    def send_logits(buf, sem):
-        rows = []
-        for part in tiles:
-            act = jnp.tanh(pre[:, part])
-            hid[:, part] = act
-            rows.append(jnp.sum(fold(act * w2[...]), axis=0, keepdims=True))
-        z_src[0] = jnp.concatenate(rows[:half_tiles], axis=0)
-        z_src[1] = jnp.concatenate(rows[half_tiles:], axis=0)
-        buf[me] = z_src[own]
-        send_halves(buf, sem)
+    def send_logits(buf, sem, update=None):
+        for half in range(2):
+            rows = []
+            for part in tiles[half * half_tiles : (half + 1) * half_tiles]:
+                if update is not None:
+                    update(part)
+                act = jnp.tanh(pre[:, part])
+                hid[:, part] = act
+                rows.append(jnp.sum(fold(act * w2[...]), axis=0, keepdims=True))
+            z_mine = jnp.concatenate(rows, axis=0)
+            z_src[half] = z_mine
+            buf[half, me] = z_mine
+            send_all(z_src.at[half], buf.at[half], sem + half, peers[:far])
+        for half in range(2):
+            send_all(z_src.at[half], buf.at[half], sem + half, peers[far:])
         w2s = w2[...] * out_scale
         for part in tiles:
             act = hid[:, part]
             fac[:, part] = w2s * (1.0 - act * act)
 
     def gram_times(buf, sem, on_tile, after_tiles, finish):
-        wait_all(buf, sem)
-        logits = jnp.sum(buf[...], axis=0) * out_scale
-        half_src[...] = logits
-        half_buf[own] = logits
-        swap = pltpu.make_async_remote_copy(
-            src_ref=half_src, dst_ref=half_buf.at[own], send_sem=send_sem.at[3], recv_sem=recv_sem.at[3],
-            device_id={axis: partner}, device_id_type=MESH,
-        )
-        swap.start()
-        for slot, half in enumerate((own, 1 - own)):
-            if slot:
-                swap.wait()
-                logits = half_buf[half]
+        for half in range(2):
+            wait_all(buf.at[half], sem + half)
+            logits = jnp.sum(buf[half], axis=0) * out_scale
+            logits_v[half] = logits
             res = (jax.nn.sigmoid(logits) - t_ref[half]) * (1.0 / num_rows)
             resid[half] = res
-            parts = []
-            for idx in range(half_tiles):
-                part = pl.ds(pl.multiple_of(half * half_rows + idx * LANES, LANES), LANES)
-                parts.append(part)
-                diff = on_tile(part, fac[:, part] * res[idx : idx + 1, :])
-                for row, term in enumerate(split3(diff)):
-                    split_d[slot, row * hid_rows : (row + 1) * hid_rows, idx * LANES : (idx + 1) * LANES] = term
+            parts = tiles[half * half_tiles : (half + 1) * half_tiles]
+            for idx, part in enumerate(parts):
+                store_split(split_d, part, on_tile(part, fac[:, part] * res[idx : idx + 1, :]))
             after_tiles(parts)
-            rows = pl.ds(pl.multiple_of(half * half_rows, half_rows), half_rows)
+            rows = pl.ds(half * half_rows, half_rows)
             for part in row_parts:
-                high = jnp.dot(split_d[slot], gram[0, rows, part], preferred_element_type=F32)
-                mid = jnp.dot(split_d[slot, : 2 * hid_rows], gram[1, rows, part], preferred_element_type=F32)
-                low = jnp.dot(split_d[slot, :hid_rows], gram[2, rows, part], preferred_element_type=F32)
+                high = jnp.dot(split_d[:, rows], gram[0, rows, part], preferred_element_type=F32)
+                mid = jnp.dot(split_d[: 2 * hid_rows, rows], gram[1, rows, part], preferred_element_type=F32)
+                low = jnp.dot(split_d[:hid_rows, rows], gram[2, rows, part], preferred_element_type=F32)
                 small = (high[2 * hid_rows :] + mid[hid_rows:]) + low
                 total = ((high[hid_rows : 2 * hid_rows] + mid[:hid_rows]) + small) + high[:hid_rows]
-                if slot:
+                if half:
                     finish(part, ((total + k_part[:, part]) * x_scale) * x_scale)
                 else:
                     k_part[:, part] = total
@@ -193,14 +178,11 @@
 
     def keep_g_part(idx):
         for part in col_parts:
-            prods = []
-            for slot, half in enumerate((own, 1 - own)):
-                rows = pl.ds(pl.multiple_of(half * half_rows, half_rows), half_rows)
-                prods.append(jnp.dot(split_d[slot], xs[rows, part], preferred_element_type=F32))
-            g_parts[idx, :, part] = merge3(prods[0] + prods[1], hid_rows) * in_scale * x_scale
+            prod = jnp.dot(split_d[...], xs[:, part], preferred_element_type=F32)
+            g_parts[idx, :, part] = merge3(prod, hid_rows) * in_scale * x_scale
 
     def store_loss(idx):
-        logits = half_buf[...]
+        logits = logits_v[...]
         soft = jnp.maximum(logits, 0.0) + jnp.log1p(jnp.exp(-jnp.abs(logits)))
         out_loss[idx] = jnp.sum(soft - t_ref[...] * logits) * (1.0 / num_rows)
 
@@ -222,10 +204,13 @@
         s_part = combine(cfs, slots, m_g, m_s, m_y, w2rows, lanes)
         m_s[new, w2rows, :] = s_part
         w2[...] = w2[...] + s_part
-        for part in tiles:
+
+        def update(part):
             q_part = combine(cfs, slots, q_g, q_s, q_y, every, part)
             q_s[new, :, part] = q_part
             pre[:, part] = pre[:, part] + q_part
+
+        return update
 
     def move_rest(cfs, slots):
         new = slots[-1]
@@ -266,7 +251,7 @@
             q_g[:, part] = q_g[:, part] + q_new
             rest["yy"] = rest["yy"] + fold(d_y[new, :, part] * q_new)
 
-        gram_times(z_buf.at[1], 1, on_tile, after_tiles, finish)
+        gram_times(z_buf.at[1], 2, on_tile, after_tiles, finish)
         w2_part = w2_grad() - m_g[w2rows, :]
         w0_y = reg * m_s[new, sums, :] + rest["w0"]
         cf_y = reg * m_s[new, cfrow, :] + jnp.where(unit == k + 1, 1.0, 0.0)
@@ -284,14 +269,14 @@
         packed = jnp.sum(jnp.where(eye[:NUM_DOTS], totals, 0.0), axis=0, keepdims=True)
         dot_src[...] = packed
         dot_buf[me] = packed
-        send_all(dot_src, dot_buf, 2)
+        send_all(dot_src, dot_buf, 4)
         m_g[...] = m_g[...] + m_y[new]
         for part in tiles:
             d_g[:, part] = d_g[:, part] + d_y[new, :, part]
 
     def two_loop(carry):
         rho1, rho2, psg0, psg1, pyg0, pyg1, pys1, yy11, yy12, yy22 = carry
-        wait_all(dot_buf, 2)
+        wait_all(dot_buf, 4)
         total = jnp.sum(dot_buf[...], axis=0)
         ys0, ys1, ys2, yy0, yy1, yy2, ygp, gs0 = (
             jnp.broadcast_to(total[:, idx : idx + 1], (SUBL, LANES)) for idx in range(NUM_DOTS)
@@ -376,8 +361,7 @@
         new, old1, old2 = lax.rem(k, HIST), lax.rem(k + 2, HIST), lax.rem(k + 1, HIST)
         prev = (old1, old2, new)
         cfs = load_coef()
-        move(cfs, prev)
-        send_logits(z_buf.at[1], 1)
+        send_logits(z_buf.at[1], 2, move(cfs, prev))
         acc_gs = move_rest(cfs, prev)
         keep_g_part(k - 1)
         new_grad(k, (new, old1, old2), acc_gs)
@@ -473,21 +457,20 @@
                 pltpu.VMEM((meta, LANES), F32),
                 pltpu.VMEM((hid_rows, LANES), F32),
                 pltpu.VMEM((SUBL, LANES), F32),
-                pltpu.VMEM((2, 3 * hid_rows, num_rows // 2), BF16),
+                pltpu.VMEM((3 * hid_rows, num_rows), BF16),
                 pltpu.VMEM((3 * hid_rows, dim), BF16),
                 halves,
                 flat,
                 pltpu.VMEM((1 + 2 * HIST, SUBL, LANES), F32),
                 halves,
-                pltpu.VMEM((2, n, row_tiles // 2, LANES), F32),
-                pltpu.VMEM((row_tiles // 2, LANES), F32),
+                pltpu.VMEM((2, 2, n, row_tiles // 2, LANES), F32),
                 halves,
                 pltpu.VMEM((1, LANES), F32),
                 pltpu.VMEM((n, 1, LANES), F32),
                 pltpu.SemaphoreType.DMA((1 + num_rows // ROW_CHUNK,)),
                 pltpu.SemaphoreType.DMA((4,)),
-                pltpu.SemaphoreType.DMA((4,)),
-                pltpu.SemaphoreType.DMA((4,)),
+                pltpu.SemaphoreType.DMA((5,)),
+                pltpu.SemaphoreType.DMA((5,)),
             ],
             compiler_params=pltpu.CompilerParams(
                 collective_id=0, has_side_effects=True, vmem_limit_bytes=46 * 1024 * 1024

time: 85.8 us -> 84.6 us (0.986)
  Pallas kernels: 83.6 us -> 82.4 us
    pallas_call x1, Pallas kernels: 82.2 us -> 80.9 us  [local_solve(): pl.pallas_call(functools.partial(kernel, 'feat', n, in_scale, out_scale),...]
where the time goes in v7:
time: 84.6 us; the launch traced here: 84.5 us
  Pallas kernels  82.4 us (97%)
  between operations  2.09 us (2%)
    pallas_call x1, Pallas kernels, local_solve(): pl.pallas_call(functools.partial(kernel, 'feat', n, in_scale, out_scale),...  80.9 us

profile of v7, /device:TPU:21, one launch (start us, length us, event | category | flops | bytes accessed | tf_op | source)
XLA Modules:
  0.0 84.5 jit_solution(17576560270516704266)
XLA Ops:
  1.9 80.9 %shard_map.85 = (f32[128,3200]{1,0:T(8,128)S(1)}, f32[6,128,3200]{2,1,0:T(8,128)S(1)}, f32[7,8,128]{2,1,0:T(8,128)S(1)}, f32[1,128]{1,0:T(1,128)S(1)}, f32[6]{0:T(128)S(4)}) custom-call(bf16[1024,3072]{1,0:T(8,128)(2,1)} %x_hbm.1, f32[2,4,128]{2,1,0:T(4,128)} %bitcast.3, f32[128,3072]{1,0:T(8,128)} %win_hbm.1, f32[1,128]{1,0:T(1,128)} %bitcast.4, ...), custom_call_target="tpu_custom_call" | custom-call | tf_op jit(solution)/shard_map/pallas_call | solution.py:434
  82.9 1.4 %shard_map.86 = (f32[128,3072]{1,0:T(8,128)}, f32[1,128]{1,0:T(1,128)}, f32[6]{0:T(128)}) custom-call(f32[128,3200]{1,0:T(8,128)S(1)} %get-tuple-element.11.w0, f32[6,128,3200]{2,1,0:T(8,128)S(1)} %get-tuple-element.12.g_parts, f32[7,8,128]{2,1,0:T(8,128)S(1)} %get-tuple-element.13.weights, f32[1,128]{1,0:T(1,128)S(1)} %get-tuple-element.14.w2_ref, ...), custom_call_target="tpu_custom_call" | custom-call | tf_op jit(solution)/shard_map/pallas_call | solution.py:485

commit v8 on v4

--- a/solution.py
+++ b/solution.py
@@ -14,6 +14,7 @@
 SUBL = 8
 ROW_CHUNK = 512
 COL_CHUNK = 512
+G_TRIPS = 3
 NUM_DOTS = 8
 MESH = pl.DeviceIdType.MESH
 F32 = jnp.float32
@@ -157,7 +158,11 @@
         return (((high[hid_rows : 2 * hid_rows] + mid[:hid_rows]) + small + high[:hid_rows]) * x_scale) * x_scale
 
     def keep_g_part(idx):
-        for part in col_parts:
+        width = dim // G_TRIPS
+
+        @pl.loop(0, G_TRIPS)
+        def _(trip):
+            part = pl.ds(pl.multiple_of(trip * width, width), width)
             prod = jnp.dot(split_d[...], xs[:, part], preferred_element_type=F32)
             g_parts[idx, :, part] = merge3(prod, hid_rows) * in_scale * x_scale
 
@@ -337,19 +342,21 @@
         residual(z_buf.at[1], 1)
         new_grad(k, (new, old1, old2), acc_gs)
 
+    last = NUM_ITERS - 1
+
     def body(k, carry):
         head(k)
         store_loss(k)
+
+        @pl.when(k == last)
+        def _():
+            keep_g_part(last)
+
         return two_loop(carry)
 
     zero = jnp.zeros((SUBL, LANES), F32)
-    carry = lax.fori_loop(1, NUM_ITERS - 1, body, (zero,) * 10)
-
-    last = NUM_ITERS - 1
-    head(last)
-    store_loss(last)
-    keep_g_part(last)
-    two_loop(carry)
+    lax.fori_loop(1, NUM_ITERS, body, (zero,) * 10)
+
     slots = (last % HIST, (last + 2) % HIST, (last + 1) % HIST)
     cfs = load_coef()
     w2_new = w2[...] + combine(cfs, slots, m_g, m_s, m_y, w2rows, lanes)

time: 84 us -> 85.3 us (1.015)
  Pallas kernels: 81.7 us -> 83.1 us
    pallas_call x1, Pallas kernels: 80.3 us -> 81.6 us  [local_solve(): pl.pallas_call(functools.partial(kernel, 'feat', n, in_scale, out_scale),...]
where the time goes in v8:
time: 85.3 us; the launch traced here: 85.2 us
  Pallas kernels  83.1 us (97%)
  between operations  2.09 us (2%)
    pallas_call x1, Pallas kernels, local_solve(): pl.pallas_call(functools.partial(kernel, 'feat', n, in_scale, out_scale),...  81.6 us

profile of v8, /device:TPU:21, one launch (start us, length us, event | category | flops | bytes accessed | tf_op | source)
XLA Modules:
  0.0 85.2 jit_solution(8803208367639497006)
XLA Ops:
  1.9 81.6 %shard_map.85 = (f32[128,3200]{1,0:T(8,128)S(1)}, f32[6,128,3200]{2,1,0:T(8,128)S(1)}, f32[7,8,128]{2,1,0:T(8,128)S(1)}, f32[1,128]{1,0:T(1,128)S(1)}, f32[6]{0:T(128)S(4)}) custom-call(bf16[1024,3072]{1,0:T(8,128)(2,1)} %x_hbm.1, f32[8,128]{1,0:T(8,128)} %bitcast.3, f32[128,3072]{1,0:T(8,128)} %win_hbm.1, f32[1,128]{1,0:T(1,128)} %bitcast.4, ...), custom_call_target="tpu_custom_call" | custom-call | tf_op jit(solution)/shard_map/pallas_call | solution.py:411
  83.6 1.4 %shard_map.86 = (f32[128,3072]{1,0:T(8,128)}, f32[1,128]{1,0:T(1,128)}, f32[6]{0:T(128)}) custom-call(f32[128,3200]{1,0:T(8,128)S(1)} %get-tuple-element.11.w0, f32[6,128,3200]{2,1,0:T(8,128)S(1)} %get-tuple-element.12.g_parts, f32[7,8,128]{2,1,0:T(8,128)S(1)} %get-tuple-element.13.weights, f32[1,128]{1,0:T(1,128)S(1)} %get-tuple-element.14.w2_ref, ...), custom_call_target="tpu_custom_call" | custom-call | tf_op jit(solution)/shard_map/pallas_call | solution.py:461

commit v9 on v8

--- a/solution.py
+++ b/solution.py
@@ -76,12 +76,15 @@
 
     w_load = pltpu.make_async_copy(win_hbm, w0.at[:, pl.ds(0, dim)], load_sem.at[0])
     w_load.start()
+    row_parts = [pl.ds(start, ROW_CHUNK) for start in range(0, num_rows, ROW_CHUNK)]
+    dim_halves = [pl.ds(0, dim // 2), pl.ds(dim // 2, dim // 2)]
     x_loads = []
-    row_parts = [pl.ds(start, ROW_CHUNK) for start in range(0, num_rows, ROW_CHUNK)]
-    for idx, part in enumerate(row_parts):
-        load = pltpu.make_async_copy(x_hbm.at[part], x_v.at[part], load_sem.at[1 + idx])
+    for part in row_parts:
+        for half in dim_halves:
+            sem = load_sem.at[1 + len(x_loads)]
+            x_loads.append(pltpu.make_async_copy(x_hbm.at[part, half], x_v.at[part, half], sem))
+    for load in x_loads[:2]:
         load.start()
-        x_loads.append(load)
     smalls = []
     for idx, (src, dst) in enumerate(((t_hbm, t_ref), (wout_hbm, wout_ref), (reg_hbm, reg_ref), (step_hbm, step_ref))):
         load = pltpu.make_async_copy(src, dst, small_sem.at[idx])
@@ -92,6 +95,9 @@
     for peer in peers:
         pl.semaphore_signal(barrier, inc=1, device_id={axis: peer}, device_id_type=MESH)
 
+    w_load.wait()
+    for load in x_loads[2:]:
+        load.start()
     for load in smalls:
         load.wait()
     reg = reg_ref[0]
@@ -122,7 +128,13 @@
         for idx, term in enumerate(split3(val)):
             ref[idx * hid_rows : (idx + 1) * hid_rows, part] = term
 
-    def send_logits(buf, sem):
+    def set_factor():
+        w2s = w2[...] * out_scale
+        for part in tiles:
+            act = hid[:, part]
+            fac[:, part] = w2s * (1.0 - act * act)
+
+    def send_logits(buf, sem, lazy=False):
         rows = []
         for part in tiles:
             act = jnp.tanh(pre[:, part])
@@ -132,10 +144,8 @@
         z_src[...] = z_mine
         buf[me] = z_mine
         send_all(z_src, buf, sem)
-        w2s = w2[...] * out_scale
-        for part in tiles:
-            act = hid[:, part]
-            fac[:, part] = w2s * (1.0 - act * act)
+        if not lazy:
+            set_factor()
 
     def residual(buf, sem):
         wait_all(buf, sem)
@@ -281,7 +291,6 @@
     w2_row = jnp.broadcast_to(wout_ref[...], (hid_rows, LANES))
     w2_col = jnp.sum(jnp.where(eye, w2_row, 0.0), axis=1, keepdims=True)
     w2[...] = jnp.broadcast_to(w2_col, (hid_rows, LANES))
-    w_load.wait()
     w0_w0 = jnp.zeros((SUBL, LANES), F32)
     for start in range(0, dim, LANES):
         part = pl.ds(start, LANES)
@@ -290,19 +299,22 @@
         store_split(split_w, part, w_part)
     peaks = []
     for idx, part in enumerate(row_parts):
-        x_loads[idx].wait()
-        x_part = x_v[part, :]
-        prod = lax.dot_general(split_w[...], x_part, (((1,), (1,)), ((), ())), preferred_element_type=F32)
-        pre_part = merge3(prod, hid_rows) * in_scale
+        total = None
+        for half, load in zip(dim_halves, x_loads[2 * idx : 2 * idx + 2]):
+            load.wait()
+            prod = lax.dot_general(
+                split_w[:, half], x_v[part, half], (((1,), (1,)), ((), ())), preferred_element_type=F32
+            )
+            total = merge3(prod, hid_rows) if total is None else total + merge3(prod, hid_rows)
+        pre_part = total * in_scale
         pre[:, part] = pre_part
         pre0[:, part] = pre_part
-        peaks.append(jnp.max(jnp.abs(x_part).reshape(ROW_CHUNK // 16, 16, dim), axis=0))
+        peaks.append(jnp.max(jnp.abs(x_v[part, :]).reshape(ROW_CHUNK // 16, 16, dim), axis=0))
+    x_scale, x_inverse = power_of_two(jnp.max(functools.reduce(jnp.maximum, peaks).astype(F32)))
     pl.semaphore_wait(barrier, n - 1)
-    send_logits(z_buf.at[0], 0)
-    x_scale, x_inverse = power_of_two(jnp.max(functools.reduce(jnp.maximum, peaks).astype(F32)))
-    for part in row_parts:
-        xs[part, :] = x_v[part, :] * jnp.full((ROW_CHUNK, dim), x_inverse, F32).astype(BF16)
+    send_logits(z_buf.at[0], 0, lazy=True)
     for row, row_part in enumerate(row_parts):
+        xs[row_part, :] = x_v[row_part, :] * jnp.full((ROW_CHUNK, dim), x_inverse, F32).astype(BF16)
         for col, col_part in enumerate(row_parts[: row + 1]):
             block = lax.dot_general(
                 xs[row_part, :], xs[col_part, :], (((1,), (1,)), ((), ())), preferred_element_type=F32
@@ -312,6 +324,7 @@
             if col < row:
                 for idx, term in enumerate(split3(block.T)):
                     gram[idx, col_part, row_part] = term
+    set_factor()
     for ref in (q_s, q_y, d_s, d_y, m_s, m_y, coef):
         ref[...] = jnp.zeros_like(ref)
     cv[...] = jnp.where(unit == 0, 1.0, 0.0)
@@ -443,7 +456,7 @@
                 pltpu.VMEM((2, n, row_tiles, LANES), F32),
                 pltpu.VMEM((1, LANES), F32),
                 pltpu.VMEM((n, 1, LANES), F32),
-                pltpu.SemaphoreType.DMA((1 + num_rows // ROW_CHUNK,)),
+                pltpu.SemaphoreType.DMA((1 + 2 * (num_rows // ROW_CHUNK),)),
                 pltpu.SemaphoreType.DMA((4,)),
                 pltpu.SemaphoreType.DMA((3,)),
                 pltpu.SemaphoreType.DMA((3,)),

time: 85.3 us -> 85.7 us (level)
  no operation moved by 1% of the time
where the time goes in v9:
time: 85.7 us; the launch traced here: 85.6 us
  Pallas kernels  83.5 us (97%)
  between operations  2.09 us (2%)
    pallas_call x1, Pallas kernels, local_solve(): pl.pallas_call(functools.partial(kernel, 'feat', n, in_scale, out_scale),...  82.1 us

profile of v9, /device:TPU:21, one launch (start us, length us, event | category | flops | bytes accessed | tf_op | source)
XLA Modules:
  0.0 85.6 jit_solution(5233549729221018322)
XLA Ops:
  1.9 82.1 %shard_map.85 = (f32[128,3200]{1,0:T(8,128)S(1)}, f32[6,128,3200]{2,1,0:T(8,128)S(1)}, f32[7,8,128]{2,1,0:T(8,128)S(1)}, f32[1,128]{1,0:T(1,128)S(1)}, f32[6]{0:T(128)S(4)}) custom-call(bf16[1024,3072]{1,0:T(8,128)(2,1)} %x_hbm.1, f32[8,128]{1,0:T(8,128)} %bitcast.3, f32[128,3072]{1,0:T(8,128)} %win_hbm.1, f32[1,128]{1,0:T(1,128)} %bitcast.4, ...), custom_call_target="tpu_custom_call" | custom-call | tf_op jit(solution)/shard_map/pallas_call | solution.py:424
  84.0 1.4 %shard_map.86 = (f32[128,3072]{1,0:T(8,128)}, f32[1,128]{1,0:T(1,128)}, f32[6]{0:T(128)}) custom-call(f32[128,3200]{1,0:T(8,128)S(1)} %get-tuple-element.11.w0, f32[6,128,3200]{2,1,0:T(8,128)S(1)} %get-tuple-element.12.g_parts, f32[7,8,128]{2,1,0:T(8,128)S(1)} %get-tuple-element.13.weights, f32[1,128]{1,0:T(1,128)S(1)} %get-tuple-element.14.w2_ref, ...), custom_call_target="tpu_custom_call" | custom-call | tf_op jit(solution)/shard_map/pallas_call | solution.py:474

commit v10 on v9

--- a/solution.py
+++ b/solution.py
@@ -14,7 +14,6 @@
 SUBL = 8
 ROW_CHUNK = 512
 COL_CHUNK = 512
-G_TRIPS = 3
 NUM_DOTS = 8
 MESH = pl.DeviceIdType.MESH
 F32 = jnp.float32
@@ -168,11 +167,7 @@
         return (((high[hid_rows : 2 * hid_rows] + mid[:hid_rows]) + small + high[:hid_rows]) * x_scale) * x_scale
 
     def keep_g_part(idx):
-        width = dim // G_TRIPS
-
-        @pl.loop(0, G_TRIPS)
-        def _(trip):
-            part = pl.ds(pl.multiple_of(trip * width, width), width)
+        for part in col_parts:
             prod = jnp.dot(split_d[...], xs[:, part], preferred_element_type=F32)
             g_parts[idx, :, part] = merge3(prod, hid_rows) * in_scale * x_scale
 
@@ -355,21 +350,19 @@
         residual(z_buf.at[1], 1)
         new_grad(k, (new, old1, old2), acc_gs)
 
-    last = NUM_ITERS - 1
-
     def body(k, carry):
         head(k)
         store_loss(k)
-
-        @pl.when(k == last)
-        def _():
-            keep_g_part(last)
-
         return two_loop(carry)
 
     zero = jnp.zeros((SUBL, LANES), F32)
-    lax.fori_loop(1, NUM_ITERS, body, (zero,) * 10)
-
+    carry = lax.fori_loop(1, NUM_ITERS - 1, body, (zero,) * 10)
+
+    last = NUM_ITERS - 1
+    head(last)
+    store_loss(last)
+    keep_g_part(last)
+    two_loop(carry)
     slots = (last % HIST, (last + 2) % HIST, (last + 1) % HIST)
     cfs = load_coef()
     w2_new = w2[...] + combine(cfs, slots, m_g, m_s, m_y, w2rows, lanes)

time: 85.7 us -> 84.1 us (0.981)
  Pallas kernels: 83.5 us -> 81.3 us
    pallas_call x1, Pallas kernels: 82.1 us -> 79.9 us  [local_solve(): pl.pallas_call(functools.partial(kernel, 'feat', n, in_scale, out_scale),...]
where the time goes in v10:
time: 84.1 us; the launch traced here: 83.4 us
  Pallas kernels  81.3 us (97%)
  between operations  2.09 us (2%)
    pallas_call x1, Pallas kernels, local_solve(): pl.pallas_call(functools.partial(kernel, 'feat', n, in_scale, out_scale),...  79.9 us

profile of v10, /device:TPU:21, one launch (start us, length us, event | category | flops | bytes accessed | tf_op | source)
XLA Modules:
  0.0 83.4 jit_solution(1212626406171677659)
XLA Ops:
  1.9 79.9 %shard_map.85 = (f32[128,3200]{1,0:T(8,128)S(1)}, f32[6,128,3200]{2,1,0:T(8,128)S(1)}, f32[7,8,128]{2,1,0:T(8,128)S(1)}, f32[1,128]{1,0:T(1,128)S(1)}, f32[6]{0:T(128)S(4)}) custom-call(bf16[1024,3072]{1,0:T(8,128)(2,1)} %x_hbm.1, f32[8,128]{1,0:T(8,128)} %bitcast.3, f32[128,3072]{1,0:T(8,128)} %win_hbm.1, f32[1,128]{1,0:T(1,128)} %bitcast.4, ...), custom_call_target="tpu_custom_call" | custom-call | tf_op jit(solution)/shard_map/pallas_call | solution.py:417
  81.8 1.4 %shard_map.86 = (f32[128,3072]{1,0:T(8,128)}, f32[1,128]{1,0:T(1,128)}, f32[6]{0:T(128)}) custom-call(f32[128,3200]{1,0:T(8,128)S(1)} %get-tuple-element.11.w0, f32[6,128,3200]{2,1,0:T(8,128)S(1)} %get-tuple-element.12.g_parts, f32[7,8,128]{2,1,0:T(8,128)S(1)} %get-tuple-element.13.weights, f32[1,128]{1,0:T(1,128)S(1)} %get-tuple-element.14.w2_ref, ...), custom_call_target="tpu_custom_call" | custom-call | tf_op jit(solution)/shard_map/pallas_call | solution.py:467

commit v11 on v10

--- a/solution.py
+++ b/solution.py
@@ -287,15 +287,22 @@
     w2_col = jnp.sum(jnp.where(eye, w2_row, 0.0), axis=1, keepdims=True)
     w2[...] = jnp.broadcast_to(w2_col, (hid_rows, LANES))
     w0_w0 = jnp.zeros((SUBL, LANES), F32)
-    for start in range(0, dim, LANES):
-        part = pl.ds(start, LANES)
-        w_part = w0[:, part]
-        w0_w0 = w0_w0 + fold(w_part * w_part)
-        store_split(split_w, part, w_part)
+
+    def split_half(first, acc):
+        for start in range(first, first + dim // 2, LANES):
+            part = pl.ds(start, LANES)
+            w_part = w0[:, part]
+            acc = acc + fold(w_part * w_part)
+            store_split(split_w, part, w_part)
+        return acc
+
+    w0_w0 = split_half(0, w0_w0)
     peaks = []
     for idx, part in enumerate(row_parts):
         total = None
         for half, load in zip(dim_halves, x_loads[2 * idx : 2 * idx + 2]):
+            if idx == 0 and total is not None:
+                w0_w0 = split_half(dim // 2, w0_w0)
             load.wait()
             prod = lax.dot_general(
                 split_w[:, half], x_v[part, half], (((1,), (1,)), ((), ())), preferred_element_type=F32

time: 84.1 us -> 85.1 us (1.012)
  no operation moved by 1% of the time
where the time goes in v11:
time: 85.1 us; the launch traced here: 83.6 us
  Pallas kernels  81.5 us (96%)
  between operations  2.09 us (2%)
    pallas_call x1, Pallas kernels, local_solve(): pl.pallas_call(functools.partial(kernel, 'feat', n, in_scale, out_scale),...  80.1 us

profile of v11, /device:TPU:21, one launch (start us, length us, event | category | flops | bytes accessed | tf_op | source)
XLA Modules:
  0.0 83.6 jit_solution(8980068456842669035)
XLA Ops:
  1.9 80.1 %shard_map.85 = (f32[128,3200]{1,0:T(8,128)S(1)}, f32[6,128,3200]{2,1,0:T(8,128)S(1)}, f32[7,8,128]{2,1,0:T(8,128)S(1)}, f32[1,128]{1,0:T(1,128)S(1)}, f32[6]{0:T(128)S(4)}) custom-call(bf16[1024,3072]{1,0:T(8,128)(2,1)} %x_hbm.1, f32[8,128]{1,0:T(8,128)} %bitcast.3, f32[128,3072]{1,0:T(8,128)} %win_hbm.1, f32[1,128]{1,0:T(1,128)} %bitcast.4, ...), custom_call_target="tpu_custom_call" | custom-call | tf_op jit(solution)/shard_map/pallas_call | solution.py:424
  82.0 1.4 %shard_map.86 = (f32[128,3072]{1,0:T(8,128)}, f32[1,128]{1,0:T(1,128)}, f32[6]{0:T(128)}) custom-call(f32[128,3200]{1,0:T(8,128)S(1)} %get-tuple-element.11.w0, f32[6,128,3200]{2,1,0:T(8,128)S(1)} %get-tuple-element.12.g_parts, f32[7,8,128]{2,1,0:T(8,128)S(1)} %get-tuple-element.13.weights, f32[1,128]{1,0:T(1,128)S(1)} %get-tuple-element.14.w2_ref, ...), custom_call_target="tpu_custom_call" | custom-call | tf_op jit(solution)/shard_map/pallas_call | solution.py:474
